TPU v7x, 256 devices: a whole 4x4x8 slice. The times are simulated.
256 devices in a mesh: seq: 64 (over x, z, core), head: 4 (over y).
Axes of the slice: x: 4, y: 4, z: 8, core: 2. Of those that a mesh axis runs over, the one named last changes fastest.
Arguments:
- queries: bfloat16 [65536, 1536], P('seq', 'head'), may hold values from -5 to 5
- key_vectors: bfloat16 [65536, 1536], P('seq', 'head'), may hold values from -5 to 5
- value_vectors: bfloat16 [65536, 1536], P('seq', 'head'), may hold values from -6 to 6
- out_grad: bfloat16 [65536, 1536], P('seq', 'head'), may hold values from -6 to 6
- gate_logit: float32 [12], P('head'), may hold values from -2 to 2
- doc_index: int32 [64], replicated, may hold values from 0 to 3, never falling along the last dimension, each value on 1 to 32 neighbouring positions
Outputs:
- query_grad: float32 [65536, 1536], P('seq', 'head')
- key_grad: float32 [65536, 1536], P('seq', 'head')
- value_grad: float32 [65536, 1536], P('seq', 'head')
- gate_grad: float32 [12], P('head')
Inputs may be any that keep to these rules, and one draw needn't show every extreme that they name: `doc_index`: never falls from one segment to the next; every document holds 1 to 32 segments, and one holds exactly 32.
All inputs are finite; a program needn't handle non-finite values.
Results may differ from a plain program's by a relative error of at most 0.0017.
The roundings to bfloat16 on the way count: a program that leaves them out, or rounds other values in their place, can miss the bound.
Values sent between devices are 32-bit elements; how exact they have to be, the bound alone decides.
A program may use at most 128 MiB of HBM per device.

v0:
```python
import jax
import jax.numpy as jnp
from jax import lax
from jax.sharding import Mesh
from jax.sharding import PartitionSpec as P

SEQ = ("seq_0", "seq_1", "seq_2")


def nothing_yet(value, identity):
    return jax.tree.map(
        lambda a, e: jnp.broadcast_to(jnp.asarray(e, a.dtype), a.shape), value, identity
    )


def gathered_once(value, axis):
    leaves = jax.tree.leaves(value)
    sequence = sorted(range(len(leaves)), key=lambda k: -leaves[k].size)
    width = (1, *leaves[sequence[0]].shape)[-1]
    lines = [
        jnp.pad(leaves[k].reshape(-1), (0, -leaves[k].size % width)).reshape(-1, width)
        for k in sequence
    ]
    both, at, found = (lax.all_gather(jnp.concatenate(lines), axis), 0, {})
    for k, line in zip(sequence, lines):
        share = both[:, at : at + len(line)].reshape(len(both), -1)
        found[k] = share[:, : leaves[k].size].reshape(-1, *leaves[k].shape)
        at += len(line)
    numbers = iter(range(len(leaves)))
    return jax.tree.map(lambda _: found[next(numbers)], value)


def prefix_by_axis(value, axes, combine, identity):
    before = start = nothing_yet(value, identity)
    running = value
    for axis in reversed(axes):
        size, position = (lax.axis_size(axis), lax.axis_index(axis))
        pieces = gathered_once(running, axis)
        inside, running = (start, start)
        for k in range(size):
            passed = k < position
            running = combine(running, jax.tree.map(lambda part: part[k], pieces))
            inside = jax.tree.map(lambda new, old: jnp.where(passed, new, old), running, inside)
        before = combine(inside, before)
    return before


def collected_alike(value, axis):
    leaves, found = (jax.tree.leaves(value), {})
    for leading, a in enumerate(leaves):
        if leading not in found:
            alike = [k for k, b in enumerate(leaves) if b.dtype == a.dtype]
            got = (
                gathered_once([leaves[k] for k in alike], axis)
                if len(alike) > 1
                else [lax.all_gather(a, axis)]
            )
            for k, b in zip(alike, got):
                found[k] = b
    numbers = iter(range(len(leaves)))
    return jax.tree.map(lambda _: found[next(numbers)], value)


def entering(value, axes, combine, identity):
    before = start = nothing_yet(value, identity)
    running = value
    for axis in reversed(axes):
        size, position = (lax.axis_size(axis), lax.axis_index(axis))
        pieces = collected_alike(running, axis)
        inside, running = (start, start)
        for k in reversed(range(size)):
            passed = k > position
            running = combine(running, jax.tree.map(lambda part: part[k], pieces))
            inside = jax.tree.map(lambda new, old: jnp.where(passed, new, old), running, inside)
        before = combine(inside, before)
    return before


def by_axis(value, axes):
    for axis in axes:
        value = lax.psum(value, axis)
    return value


def feature(values_in):
    return jnp.where(values_in > 0, values_in + 1.0, jnp.exp(jnp.minimum(values_in, 0.0)))


def feature_slope(values_in):
    return jnp.where(values_in > 0, 1.0, jnp.exp(jnp.minimum(values_in, 0.0)))


def contribution(key_vectors, value_vectors, head_count):
    row_count = key_vectors.shape[0]
    key_feature = feature(key_vectors.astype(jnp.float32)).astype(jnp.bfloat16)
    feature_three = key_feature.reshape(row_count, head_count, -1)
    value_three = value_vectors.reshape(row_count, head_count, -1)
    memory_part = jnp.einsum(
        "nhd,nhe->hde", feature_three, value_three, preferred_element_type=jnp.float32
    )
    norm_part = jnp.sum(feature_three, axis=0, dtype=jnp.float32)
    return (memory_part, norm_part, key_feature)


def head_work(
    head_index,
    queries,
    key_vectors,
    value_vectors,
    out_grad,
    query_feature,
    memory_prev,
    norm_prev,
    gate_prob,
):
    head_size = memory_prev.shape[-1]
    row_count = queries.shape[0]

    def take_columns(matrix):
        return lax.dynamic_slice_in_dim(matrix, head_index * head_size, head_size, 1)

    query_head = take_columns(queries)
    key_head = take_columns(key_vectors)
    value_head = take_columns(value_vectors)
    grad_head = take_columns(out_grad)
    query_float = take_columns(query_feature).astype(jnp.float32)
    memory_share = gate_prob[head_index]
    local_share = 1.0 - memory_share
    score_scale = head_size ** (-0.5)
    scores = (
        lax.dot_general(
            query_head, key_head, (((1,), (1,)), ((), ())), preferred_element_type=jnp.float32
        )
        * score_scale
    )
    row_ids = lax.broadcasted_iota(jnp.int32, (row_count, row_count), 0)
    col_ids = lax.broadcasted_iota(jnp.int32, (row_count, row_count), 1)
    scores = jnp.where(row_ids >= col_ids, scores, -1e30)
    attention = jnp.exp(scores - jnp.max(scores, axis=1, keepdims=True))
    attention = attention / jnp.sum(attention, axis=1, keepdims=True)
    attention_low = attention.astype(jnp.bfloat16)
    local_read = jnp.dot(attention_low, value_head, preferred_element_type=jnp.float32)
    prob_grad = local_share * lax.dot_general(
        grad_head, value_head, (((1,), (1,)), ((), ())), preferred_element_type=jnp.float32
    )
    row_delta = jnp.sum(prob_grad * attention, axis=1, keepdims=True)
    score_grad = (attention * (prob_grad - row_delta)).astype(jnp.bfloat16)
    query_local = jnp.dot(score_grad, key_head, preferred_element_type=jnp.float32) * score_scale
    key_local = (
        lax.dot_general(
            score_grad, query_head, (((0,), (0,)), ((), ())), preferred_element_type=jnp.float32
        )
        * score_scale
    )
    value_local = local_share * lax.dot_general(
        attention_low, grad_head, (((0,), (0,)), ((), ())), preferred_element_type=jnp.float32
    )
    memory_head = memory_prev[head_index]
    norm_head = norm_prev[head_index]
    numerator = jnp.dot(query_float, memory_head, precision=lax.Precision.HIGHEST)
    denominator = 1.0 + jnp.dot(query_float, norm_head, precision=lax.Precision.HIGHEST)
    memory_read = numerator / denominator[:, None]
    grad_float = grad_head.astype(jnp.float32)
    num_grad = memory_share * grad_float / denominator[:, None]
    den_grad = -memory_share * jnp.sum(grad_float * memory_read, axis=1) / denominator
    grad_memory = lax.dot_general(
        query_float, num_grad, (((0,), (0,)), ((), ())), precision=lax.Precision.HIGHEST
    )
    grad_norm = jnp.dot(den_grad, query_float, precision=lax.Precision.HIGHEST)
    feature_grad = (
        lax.dot_general(
            num_grad, memory_head, (((1,), (1,)), ((), ())), precision=lax.Precision.HIGHEST
        )
        + den_grad[:, None] * norm_head[None, :]
    )
    query_grad = query_local + feature_grad * feature_slope(query_head.astype(jnp.float32))
    gate_part = memory_share * local_share * jnp.sum(grad_float * (memory_read - local_read))
    return (query_grad, key_local, value_local, grad_memory, grad_norm, gate_part)


def to_rows(stacked):
    return jnp.transpose(stacked, (1, 0, 2)).reshape(stacked.shape[1], -1)


def finish(
    key_vectors, value_vectors, key_feature, key_local, value_local, later_memory, later_norm
):
    row_count = key_vectors.shape[0]
    head_count = later_memory.shape[0]
    value_three = value_vectors.reshape(row_count, head_count, -1).astype(jnp.float32)
    feature_three = key_feature.reshape(row_count, head_count, -1).astype(jnp.float32)
    key_three = key_vectors.reshape(row_count, head_count, -1).astype(jnp.float32)
    feature_grad = (
        jnp.einsum("nhe,hde->nhd", value_three, later_memory, precision=lax.Precision.HIGHEST)
        + later_norm[None]
    )
    key_grad = key_local + (feature_grad * feature_slope(key_three)).reshape(row_count, -1)
    value_extra = jnp.einsum(
        "nhd,hde->nhe", feature_three, later_memory, precision=lax.Precision.HIGHEST
    )
    value_grad = value_local + value_extra.reshape(row_count, -1)
    return (key_grad, value_grad)


def segment_join(earlier, latter):
    keep_old = 1.0 - latter[0]
    return (
        jnp.maximum(earlier[0], latter[0]),
        latter[1] + keep_old * earlier[1],
        latter[2] + keep_old * earlier[2],
    )


def per_device(queries, key_vectors, value_vectors, out_grad, gate_logit, doc_index):
    head_count = gate_logit.shape[0]
    gate_prob = jax.nn.sigmoid(gate_logit)
    memory_part, norm_part, key_feature = contribution(key_vectors, value_vectors, head_count)
    shard_count = lax.axis_size(SEQ)
    position = lax.axis_index(SEQ)
    own_doc = doc_index[position]
    prev_doc = doc_index[jnp.maximum(position - 1, 0)]
    next_doc = doc_index[jnp.minimum(position + 1, shard_count - 1)]
    opening = jnp.logical_or(position == 0, prev_doc != own_doc).astype(jnp.float32)
    closing = jnp.logical_or(position == shard_count - 1, next_doc != own_doc).astype(jnp.float32)
    zero_state = (jnp.zeros_like(memory_part), jnp.zeros_like(norm_part))
    identity_value = (jnp.zeros((), jnp.float32), zero_state[0], zero_state[1])
    running = prefix_by_axis((opening, memory_part, norm_part), SEQ, segment_join, identity_value)
    memory_prev = (1.0 - opening) * running[1]
    norm_prev = (1.0 - opening) * running[2]
    query_feature = feature(queries.astype(jnp.float32)).astype(jnp.bfloat16)

    def one_head(head_index):
        return head_work(
            head_index,
            queries,
            key_vectors,
            value_vectors,
            out_grad,
            query_feature,
            memory_prev,
            norm_prev,
            gate_prob,
        )

    results = lax.map(one_head, jnp.arange(head_count, dtype=jnp.int32))
    grad_memory = results[3]
    grad_norm = results[4]
    running_back = entering((closing, grad_memory, grad_norm), SEQ, segment_join, identity_value)
    later_memory = (1.0 - closing) * running_back[1]
    later_norm = (1.0 - closing) * running_back[2]
    key_grad, value_grad = finish(
        key_vectors,
        value_vectors,
        key_feature,
        to_rows(results[1]),
        to_rows(results[2]),
        later_memory,
        later_norm,
    )
    gate_grad = by_axis(results[5], SEQ)
    return (to_rows(results[0]), key_grad, value_grad, gate_grad)


def solution(mesh):
    split = Mesh(
        mesh.devices.reshape(4, 8, 2, mesh.shape["head"]), ("seq_0", "seq_1", "seq_2", "head")
    )
    in_specs = (P(SEQ, "head"), P(SEQ, "head"), P(SEQ, "head"), P(SEQ, "head"), P("head"), P())
    out_specs = (P(SEQ, "head"), P(SEQ, "head"), P(SEQ, "head"), P("head"))
    return jax.shard_map(
        per_device, mesh=split, in_specs=in_specs, out_specs=out_specs, check_vma=False
    )
```

profile of v0, /device:TPU:8, one launch (start us, length us, event | category | flops | bytes accessed | tf_op | source)
XLA Modules:
  0.0 302.1 jit_solution(15480716931604072538)
XLA Ops:
  13.8 2.1 all-gather.6
  23.4 39.1 %all-gather.15.cloned.1.call-done = f32[8,388,128]{2,1,0:T(8,128)} async-done(((f32[1,388,128]{2,1,0:T(8,128)}), f32[8,388,128]{2,1,0:T(8,128)}) %all-gather.15.cloned.1.call-update) | async-done | bytes 1589264 | tf_op jit(solution)/shard_map/all_gather | solution.py:24
  76.7 14.9 %all-gather.8 = f32[4,388,128]{2,1,0:T(8,128)} all-gather(f32[1,388,128]{2,1,0:T(8,128)S(1)} %maximum_bitcast_fusion.2), channel_id=4, replica_groups=mesh['seq_0'=4,'seq_1'=8,'seq_2'=2,'head'=4] {'seq_0'}, dimensions={0}, use_global_device_ids=true | all-gather | bytes 993280 | tf_op jit(solution)/shard_map/all_gather | solution.py:24
  98.2 107.5 %while.20 = (s32[]{:T(128)}, f32[3,1024,128]{1,2,0:T(8,128)}, f32[3,1024,128]{1,2,0:T(8,128)}, f32[3,1024,128]{1,2,0:T(8,128)}, f32[3,128,128]{2,1,0:T(8,128)}, ...) while((s32[]{:T(128)}, f32[3,1024,128]{1,2,0:T(8,128)}, ...), condition=%wide.region_7.8_spmd, body=%wide.region_1.7_spmd.sunk | while | flops 2260860928 | bytes 79734888 | solution.py:245
  105.9 1.9 multiply_reduce_fusion.2
  112.1 2.3 fusion.158
  115.0 2.8 fusion.159
  118.8 2.9 fusion.160
  124.9 2.8 fusion.162
  129.6 3.7 %fusion.164 = f32[]{:T(128)} fusion(f32[1024,128]{0,1:T(8,128)S(1)} %copy-done.16, bf16[1024,128]{0,1:T(8,128)(2,1)S(1)} %copy-done.6, bf16[1024,384]{1,0:T(8,128)(2,1)} %get-tuple-element.406, s32[]{:T(128)S(6)} %select_n.823, f32[1024,1024]{0,1:T(8,128)} %copy-done, f32[1024]{0:T(1024)S(1)} %fusion.155, f32[1024]{0:T(1024)S(1)} %get-tuple-element.343), kind=kOutput, calls=%fused_computation.28.clone.1 | convolution fusion | flops 275251200 | bytes 5251080 | tf_op jit(solution)/shard_map/while/body/eval_jaxpr/dot_general | solution.py:142
  141.8 1.9 multiply_reduce_fusion.2
  144.8 1.7 convolution_multiply_fusion.4
  147.9 2.3 fusion.158
  150.8 2.8 fusion.159
  154.7 2.9 fusion.160
  160.8 2.7 fusion.162
  165.5 3.7 %fusion.164 = f32[]{:T(128)} fusion(f32[1024,128]{0,1:T(8,128)S(1)} %copy-done.16, bf16[1024,128]{0,1:T(8,128)(2,1)S(1)} %copy-done.6, bf16[1024,384]{1,0:T(8,128)(2,1)} %get-tuple-element.406, s32[]{:T(128)S(6)} %select_n.823, f32[1024,1024]{0,1:T(8,128)} %copy-done, f32[1024]{0:T(1024)S(1)} %fusion.155, f32[1024]{0:T(1024)S(1)} %get-tuple-element.343), kind=kOutput, calls=%fused_computation.28.clone.1 | convolution fusion | flops 275251200 | bytes 5251080 | tf_op jit(solution)/shard_map/while/body/eval_jaxpr/dot_general | solution.py:142
  177.6 1.9 multiply_reduce_fusion.2
  183.7 2.3 fusion.158
  186.7 2.8 fusion.159
  190.5 2.9 fusion.160
  196.6 2.7 fusion.162
  201.3 3.7 %fusion.164 = f32[]{:T(128)} fusion(f32[1024,128]{0,1:T(8,128)S(1)} %copy-done.16, bf16[1024,128]{0,1:T(8,128)(2,1)S(1)} %copy-done.6, bf16[1024,384]{1,0:T(8,128)(2,1)} %get-tuple-element.406, s32[]{:T(128)S(6)} %select_n.823, f32[1024,1024]{0,1:T(8,128)} %copy-done, f32[1024]{0:T(1024)S(1)} %fusion.155, f32[1024]{0:T(1024)S(1)} %get-tuple-element.343), kind=kOutput, calls=%fused_computation.28.clone.1 | convolution fusion | flops 275251200 | bytes 5251080 | tf_op jit(solution)/shard_map/while/body/eval_jaxpr/dot_general | solution.py:142
  206.7 2.1 all-gather.9
  212.8 10.1 %psum.21 = f32[3]{0:T(128)S(1)} all-reduce(f32[3]{0:T(128)S(1)} %get-tuple-element.426), channel_id=1, replica_groups=mesh['seq_0'=4,'seq_1'=8,'seq_2'=2,'head'=4] {'seq_0'}, use_global_device_ids=true, to_apply=%region_8.9 | all-reduce | flops 3 | bytes 24 | tf_op jit(solution)/shard_map/psum | solution.py:81
  222.9 16.0 %psum.22 = f32[3]{0:T(128)S(1)} all-reduce(f32[3]{0:T(128)S(1)} %psum.21), channel_id=1, replica_groups=mesh['seq_0'=4,'seq_1'=8,'seq_2'=2,'head'=4] {'seq_1'}, use_global_device_ids=true, to_apply=%region_9.10 | all-reduce | flops 3 | bytes 24 | tf_op jit(solution)/shard_map/psum | solution.py:81
  238.9 3.0 psum.23
  241.8 3.0 %copy.80 = f32[1024,384]{1,0:T(8,128)} copy(f32[1024,384]{0,1:T(8,128)} %bitcast.229) | data formatting | bytes 3145728
  245.7 5.7 %all-gather.17.cloned.1.call-done = f32[8,388,128]{2,1,0:T(8,128)} async-done(((f32[1,388,128]{2,1,0:T(8,128)}), f32[8,388,128]{2,1,0:T(8,128)}) %all-gather.17.cloned.1.call-update) | async-done | bytes 1589264 | tf_op jit(solution)/shard_map/all_gather | solution.py:24
  265.3 14.7 %all-gather.11 = f32[4,388,128]{2,1,0:T(8,128)S(1)} all-gather(f32[1,388,128]{2,1,0:T(8,128)S(1)} %maximum_bitcast_fusion.5), channel_id=7, replica_groups=mesh['seq_0'=4,'seq_1'=8,'seq_2'=2,'head'=4] {'seq_0'}, dimensions={0}, use_global_device_ids=true | all-gather | bytes 993280 | tf_op jit(solution)/shard_map/all_gather | solution.py:24
  287.0 2.9 fusion.64
  291.5 2.2 bitcast_add_fusion
  (180 shorter events, 72.4 us)
Async XLA Ops:
  7.2 5.9 %copy-start.13 = (bf16[1024,384]{1,0:T(8,128)(2,1)S(1)}, bf16[1024,384]{1,0:T(8,128)(2,1)}, u32[]{:S(2)}) copy-start(bf16[1024,384]{1,0:T(8,128)(2,1)} %param.10) | copy-start | bytes 2359300
  7.2 55.4 %all-gather.15.cloned.1.call-start = ((), (), s32[]{:S(2)}) async-start(), calls=%async_computation | async-start | bytes 1806336 | tf_op jit(solution)/shard_map/all_gather | solution.py:24
  11.4 8.6 %copy-start.9 = (bf16[1024,384]{1,0:T(8,128)(2,1)S(1)}, bf16[1024,384]{1,0:T(8,128)(2,1)}, u32[]{:S(2)}) copy-start(bf16[1024,384]{1,0:T(8,128)(2,1)} %param.8) | copy-start | bytes 2359300
  13.1 10.3 %copy-start.1 = (bf16[1024,384]{0,1:T(8,128)(2,1)}, bf16[1024,384]{0,1:T(8,128)(2,1)S(1)}, u32[]{:S(2)}) copy-start(bf16[1024,384]{0,1:T(8,128)(2,1)S(1)} %get-tuple-element.192) | copy-start | bytes 2359300
  13.1 9.0 %copy-start.15 = (f32[3]{0:T(128)S(1)}, f32[3]{0:T(128)}, u32[]{:S(2)}) copy-start(f32[3]{0:T(128)} %param.12) | copy-start | bytes 40
  13.4 63.3 %copy-start.3 = (bf16[1024,384]{0,1:T(8,128)(2,1)}, bf16[1024,384]{0,1:T(8,128)(2,1)S(1)}, u32[]{:S(2)}) copy-start(bf16[1024,384]{0,1:T(8,128)(2,1)S(1)} %copy.62) | copy-start | bytes 2359300
  15.9 4.1 %copy-start.11 = (f32[2,388,128]{2,1,0:T(8,128)}, f32[2,388,128]{2,1,0:T(8,128)S(1)}, u32[]{:S(2)}) copy-start(f32[2,388,128]{2,1,0:T(8,128)S(1)} %all-gather.6) | copy-start | bytes 1191940
  19.8 231.5 %all-gather.17.cloned.1.call-start = ((), (), s32[]{:S(2)}) async-start(), calls=%async_computation.1 | async-start | bytes 1806336 | tf_op jit(solution)/shard_map/all_gather | solution.py:24
  62.5 34.1 %copy-start.7 = (f32[8,388,128]{2,1,0:T(8,128)S(1)}, f32[8,388,128]{2,1,0:T(8,128)}, u32[]{:S(2)}) copy-start(f32[8,388,128]{2,1,0:T(8,128)} %all-gather.15.cloned.1.call-done) | copy-start | bytes 4767748
  98.2 107.5 %copy-start.14 = (f32[1,128]{1,0:T(1,128)S(1)}, f32[1,128]{1,0:T(1,128)}, u32[]{:S(2)}) copy-start(f32[1,128]{1,0:T(1,128)} %pad_bitcast_fusion.2) | copy-start | bytes 1540
  104.2 3.6 %copy-start = (f32[1024,1024]{0,1:T(8,128)}, f32[1024,1024]{0,1:T(8,128)S(1)}, u32[]{:S(2)}) copy-start(f32[1024,1024]{0,1:T(8,128)S(1)} %get-tuple-element.342) | copy-start | bytes 12582916 | tf_op jit(solution)/shard_map/while
  110.8 4.2 %copy-start.5 = (bf16[1024,128]{0,1:T(8,128)(2,1)}, bf16[1024,128]{0,1:T(8,128)(2,1)S(1)}, u32[]{:S(2)}) copy-start(bf16[1024,128]{0,1:T(8,128)(2,1)S(1)} %copy.118) | copy-start | bytes 786436 | tf_op jit(solution)/shard_map/while
  123.6 6.0 %copy-start.6 = (bf16[1024,128]{0,1:T(8,128)(2,1)S(1)}, bf16[1024,128]{0,1:T(8,128)(2,1)}, u32[]{:S(2)}) copy-start(bf16[1024,128]{0,1:T(8,128)(2,1)} %copy-done.5) | copy-start | bytes 786436 | tf_op jit(solution)/shard_map/while
  123.6 6.0 %copy-start.16 = (f32[1024,128]{0,1:T(8,128)S(1)}, f32[1024,128]{0,1:T(8,128)}, u32[]{:S(2)}) copy-start(f32[1024,128]{0,1:T(8,128)} %get-tuple-element.349) | copy-start | bytes 1572868 | tf_op jit(solution)/shard_map/while
  129.6 4.5 %copy-start.10 = (bf16[1024,384]{1,0:T(8,128)(2,1)S(1)}, bf16[1024,384]{1,0:T(8,128)(2,1)}, u32[]{:S(2)}) copy-start(bf16[1024,384]{1,0:T(8,128)(2,1)} %get-tuple-element.442) | copy-start | bytes 2359300 | tf_op jit(solution)/shard_map/while
  140.1 3.6 %copy-start = (f32[1024,1024]{0,1:T(8,128)}, f32[1024,1024]{0,1:T(8,128)S(1)}, u32[]{:S(2)}) copy-start(f32[1024,1024]{0,1:T(8,128)S(1)} %get-tuple-element.342) | copy-start | bytes 12582916 | tf_op jit(solution)/shard_map/while
  146.6 4.2 %copy-start.5 = (bf16[1024,128]{0,1:T(8,128)(2,1)}, bf16[1024,128]{0,1:T(8,128)(2,1)S(1)}, u32[]{:S(2)}) copy-start(bf16[1024,128]{0,1:T(8,128)(2,1)S(1)} %copy.118) | copy-start | bytes 786436 | tf_op jit(solution)/shard_map/while
  159.5 6.0 %copy-start.6 = (bf16[1024,128]{0,1:T(8,128)(2,1)S(1)}, bf16[1024,128]{0,1:T(8,128)(2,1)}, u32[]{:S(2)}) copy-start(bf16[1024,128]{0,1:T(8,128)(2,1)} %copy-done.5) | copy-start | bytes 786436 | tf_op jit(solution)/shard_map/while
  159.5 6.0 %copy-start.16 = (f32[1024,128]{0,1:T(8,128)S(1)}, f32[1024,128]{0,1:T(8,128)}, u32[]{:S(2)}) copy-start(f32[1024,128]{0,1:T(8,128)} %get-tuple-element.349) | copy-start | bytes 1572868 | tf_op jit(solution)/shard_map/while
  165.5 4.5 %copy-start.10 = (bf16[1024,384]{1,0:T(8,128)(2,1)S(1)}, bf16[1024,384]{1,0:T(8,128)(2,1)}, u32[]{:S(2)}) copy-start(bf16[1024,384]{1,0:T(8,128)(2,1)} %get-tuple-element.442) | copy-start | bytes 2359300 | tf_op jit(solution)/shard_map/while
  175.9 3.6 %copy-start = (f32[1024,1024]{0,1:T(8,128)}, f32[1024,1024]{0,1:T(8,128)S(1)}, u32[]{:S(2)}) copy-start(f32[1024,1024]{0,1:T(8,128)S(1)} %get-tuple-element.342) | copy-start | bytes 12582916 | tf_op jit(solution)/shard_map/while
  182.5 4.2 %copy-start.5 = (bf16[1024,128]{0,1:T(8,128)(2,1)}, bf16[1024,128]{0,1:T(8,128)(2,1)S(1)}, u32[]{:S(2)}) copy-start(bf16[1024,128]{0,1:T(8,128)(2,1)S(1)} %copy.118) | copy-start | bytes 786436 | tf_op jit(solution)/shard_map/while
  195.3 6.0 %copy-start.6 = (bf16[1024,128]{0,1:T(8,128)(2,1)S(1)}, bf16[1024,128]{0,1:T(8,128)(2,1)}, u32[]{:S(2)}) copy-start(bf16[1024,128]{0,1:T(8,128)(2,1)} %copy-done.5) | copy-start | bytes 786436 | tf_op jit(solution)/shard_map/while
  195.3 6.0 %copy-start.16 = (f32[1024,128]{0,1:T(8,128)S(1)}, f32[1024,128]{0,1:T(8,128)}, u32[]{:S(2)}) copy-start(f32[1024,128]{0,1:T(8,128)} %get-tuple-element.349) | copy-start | bytes 1572868 | tf_op jit(solution)/shard_map/while
  201.3 4.5 %copy-start.10 = (bf16[1024,384]{1,0:T(8,128)(2,1)S(1)}, bf16[1024,384]{1,0:T(8,128)(2,1)}, u32[]{:S(2)}) copy-start(bf16[1024,384]{1,0:T(8,128)(2,1)} %get-tuple-element.442) | copy-start | bytes 2359300 | tf_op jit(solution)/shard_map/while
  208.8 33.0 %copy-start.12 = (f32[2,388,128]{2,1,0:T(8,128)}, f32[2,388,128]{2,1,0:T(8,128)S(1)}, u32[]{:S(2)}) copy-start(f32[2,388,128]{2,1,0:T(8,128)S(1)} %all-gather.9) | copy-start | bytes 1191940
  244.9 42.1 %copy-start.4 = (bf16[1024,384]{0,1:T(8,128)(2,1)S(1)}, bf16[1024,384]{0,1:T(8,128)(2,1)}, u32[]{:S(2)}) copy-start(bf16[1024,384]{0,1:T(8,128)(2,1)} %copy-done.3) | copy-start | bytes 2359300
  251.4 32.8 %copy-start.8 = (f32[8,388,128]{2,1,0:T(8,128)S(1)}, f32[8,388,128]{2,1,0:T(8,128)}, u32[]{:S(2)}) copy-start(f32[8,388,128]{2,1,0:T(8,128)} %all-gather.17.cloned.1.call-done) | copy-start | bytes 4767748
  287.0 4.5 %copy-start.2 = (bf16[1024,384]{0,1:T(8,128)(2,1)S(1)}, bf16[1024,384]{0,1:T(8,128)(2,1)}, u32[]{:S(2)}) copy-start(bf16[1024,384]{0,1:T(8,128)(2,1)} %copy-done.1) | copy-start | bytes 2359300
Sparse Core Ops, SparseCore 0:
  20.0 42.5 all-gather.14
  212.9 38.4 all-gather.16
where the time goes:
time: 304 us; the launch traced here: 302 us
  matrix products  77.1 us (25%)
  blocking collectives  62.8 us (21%)
  between operations  47.7 us (16%)
  waiting for transfers between devices  44.8 us (15%)
  local copies, waits for them, and re-layouts  34.2 us (11%)
  other arithmetic  19.9 us (7%)
  loops' own time  15.5 us (5%)
    all_gather x2, waiting for transfers between devices, gathered_once(): both, at, found = (lax.all_gather(jnp.concatenate(lines), axis), 0, {})  44.8 us
    all_gather x4, blocking collectives, gathered_once(): both, at, found = (lax.all_gather(jnp.concatenate(lines), axis), 0, {})  33.8 us
    psum x3, blocking collectives, by_axis(): value = lax.psum(value, axis)  29 us
    another operation x1, loops' own time, per_device(): results = lax.map(one_head, jnp.arange(head_count, dtype=jnp.int32))  15.5 us
    dot_general x3, matrix products, head_work(): jnp.dot(attention_low, value_head, preferred_element_type=jnp.float32)  11.2 us
    dot_general x3, matrix products, head_work(): lax.dot_general(attention_low, grad_head, (((0,), (0,)), ((), ())), prefe...  8.76 us
    dot_general x3, matrix products, head_work(): lax.dot_general(num_grad, memory_head, (((1,), (1,)), ((), ())), precisio...  8.41 us
    unnamed x30, local copies, waits for them, and re-layouts  8.29 us
  transfers between devices with their start and end apart: 2, of which 2 were waited for; matrix products, arithmetic and copies ran while one was open for 2% of the time, Pallas kernels for 0%

commit v1 on v0

v1 whole, which is shorter than its diff:
```python
import functools
import math

import jax
import jax.numpy as jnp
from jax import lax
from jax.experimental import pallas as pl
from jax.experimental.pallas import tpu as pltpu
from jax.sharding import PartitionSpec as P

HD = 128
BQ = 256
F32 = jnp.float32
BF16 = jnp.bfloat16
MESH = pl.DeviceIdType.MESH
NT = (((1,), (1,)), ((), ()))
NN = (((1,), (0,)), ((), ()))
TN = (((0,), (0,)), ((), ()))


def dot(a, b, dims):
    return lax.dot_general(a, b, dims, preferred_element_type=F32)


def feature(x):
    return jnp.where(x > 0, x + 1.0, jnp.exp(jnp.minimum(x, 0.0)))


def slope(x):
    return jnp.where(x > 0, 1.0, jnp.exp(jnp.minimum(x, 0.0)))


def split(x):
    high = x.astype(BF16)
    return high, (x - high.astype(F32)).astype(BF16)


def wide(x):
    return jnp.concatenate(split(x), axis=1)


def halves(y):
    return y[:, :HD] + y[:, HD:]


def sigmoid_row(x):
    return 1.0 / (1.0 + jnp.exp(-jnp.full((1, HD), x, F32)))


def cols(h):
    if isinstance(h, int):
        return pl.ds(h * HD, HD)
    return pl.ds(pl.multiple_of(h * HD, HD), HD)


def main_kernel(
    chips,
    heads,
    doc,
    gate,
    q_hbm,
    k_hbm,
    v_hbm,
    g_hbm,
    qg,
    kl,
    vl,
    later,
    small,
    q,
    k,
    v,
    g,
    qf,
    rden,
    part,
    gpart,
    mprev,
    npart,
    nprev,
    dpart,
    local_sum,
    stage,
    pair_f,
    pair_b,
    pair_n,
    pair_d,
    send1_f,
    recv1_f,
    send2_f,
    recv2_f,
    send1_b,
    recv1_b,
    send2_b,
    recv2_b,
    send_n,
    recv_n,
    send_d,
    recv_d,
    out_f,
    out_b,
    back_f,
    back_b,
    in_sems,
    send_sems,
    recv_sems,
):
    seq = lax.axis_index("seq")
    chip, core = seq // 2, seq % 2
    partner = seq + 1 - 2 * core
    rows = heads * HD
    half = rows // 2
    page = half // chips
    tokens = q.shape[0]
    blocks = tokens // BQ

    copies = [
        pltpu.make_async_copy(src, dst, in_sems.at[n])
        for n, (src, dst) in enumerate(((k_hbm, k), (v_hbm, v), (q_hbm, q), (g_hbm, g)))
    ]
    for c in copies:
        c.start()

    barrier = pltpu.get_barrier_semaphore()
    pl.semaphore_signal(barrier, inc=1, device_id={"seq": partner}, device_id_type=MESH)

    def greet(i, carry):
        peer = 2 * lax.rem(chip + 1 + i, chips) + core
        pl.semaphore_signal(barrier, inc=1, device_id={"seq": peer}, device_id_type=MESH)
        return carry

    lax.fori_loop(0, chips - 1, greet, 0)

    def linked(s):
        before = doc[jnp.maximum(s - 1, 0)]
        return jnp.where((s > 0) & (before == doc[s]), 1.0, 0.0)

    def linked_next(s):
        after = doc[jnp.minimum(s + 1, 2 * chips - 1)]
        return jnp.where((s < 2 * chips - 1) & (after == doc[s]), 1.0, 0.0)

    same_here = linked(2 * chip + 1)

    def to_partner(src, dst, n):
        return pltpu.make_async_remote_copy(
            src_ref=src,
            dst_ref=dst,
            send_sem=send_sems.at[n],
            recv_sem=recv_sems.at[n],
            device_id={"seq": partner},
            device_id_type=MESH,
        )

    def to_chips(source, dst, n):
        def push(i, carry):
            peer = lax.rem(chip + 1 + i, chips)
            pltpu.make_async_remote_copy(
                src_ref=source(peer),
                dst_ref=dst.at[chip],
                send_sem=send_sems.at[n],
                recv_sem=recv_sems.at[n],
                device_id={"seq": 2 * peer + core},
                device_id_type=MESH,
            ).start()
            return carry

        lax.fori_loop(0, chips - 1, push, 0)

    def all_pages(buffer, n):
        rest = buffer.at[pl.ds(0, chips - 1)]
        return pltpu.make_async_remote_copy(
            src_ref=rest,
            dst_ref=rest,
            send_sem=send_sems.at[n],
            recv_sem=recv_sems.at[n],
            device_id={"seq": partner},
            device_id_type=MESH,
        )

    own_rows = pl.ds(pl.multiple_of(core * half, 8), half)
    other_rows = pl.ds(pl.multiple_of((1 - core) * half, 8), half)

    plain_f = core == 0
    plain_b = core == 1

    def joined(plain, own, received):
        return jnp.where(plain, same_here, 1.0) * own + jnp.where(plain, 1.0, same_here) * received

    def chip_value(plain, mine, pair, stage_rows, send1, recv1, n):
        stage_rows[...] = joined(plain, mine[own_rows, :], pair[...])
        for j in range(chips):
            send1[j] = stage_rows[j * page : (j + 1) * page, :]
        recv1[chip] = send1[chip]
        to_chips(lambda peer: send1.at[peer], recv1, n)

    def forward_scan(recv1, send2, recv2, n):
        all_pages(recv1, n - 1).wait_recv()

        def step(t, run):
            before = linked(2 * t) * run
            send2[t] = before
            return recv1[t] + linked(2 * t + 1) * before

        lax.fori_loop(0, chips, step, jnp.zeros((page, HD), F32))
        recv2[chip] = send2[chip]
        to_chips(lambda peer: send2.at[peer], recv2, n)

    def backward_scan(recv1, send2, recv2, n):
        all_pages(recv1, n - 1).wait_recv()

        def step(i, run):
            t = chips - 1 - i
            after = linked_next(2 * t + 1) * run
            send2[t] = after
            return recv1[t] + linked_next(2 * t) * after

        lax.fori_loop(0, chips, step, jnp.zeros((page, HD), F32))
        recv2[chip] = send2[chip]
        to_chips(lambda peer: send2.at[peer], recv2, n)

    def hand_back(plain, mine, pair, recv2, stage_rows, out, full, back, n):
        all_pages(recv2, n - 1).wait_recv()
        for j in range(chips):
            stage_rows[j * page : (j + 1) * page, :] = recv2[j]
        chip_level = stage_rows[...]
        plain_part = jnp.where(plain, mine[own_rows, :], pair[...])
        added = same_here * (chip_level + plain_part)
        full[own_rows, :] = jnp.where(plain, chip_level, added)
        out[...] = jnp.where(plain, added, chip_level)
        to_partner(out, back, n).start()

    def take_back(full, out, back, n):
        to_partner(out, back, n).wait_recv()
        full[other_rows, :] = back[...]

    PN, PF, PB, PD = 0, 1, 2, 3
    BN, BD = 4, 5
    F1, F2, F3 = 6, 7, 8
    B1, B2, B3 = 9, 10, 11

    copies[0].wait()
    copies[1].wait()
    for h in range(heads):
        key_feature = feature(k[:, cols(h)].astype(F32)).astype(BF16)
        npart[h : h + 1, :] = jnp.sum(key_feature.astype(F32), axis=0, keepdims=True)
        part[h * HD : (h + 1) * HD, :] = dot(key_feature, v[:, cols(h)], TN)

    pl.semaphore_wait(barrier, chips)
    to_partner(npart, pair_n, PN).start()
    to_partner(part.at[other_rows], pair_f, PF).start()

    copies[2].wait()
    copies[3].wait()
    for h in range(heads):
        qf[:, cols(h)] = feature(q[:, cols(h)].astype(F32)).astype(BF16)

    to_partner(npart, pair_n, PN).wait_recv()
    send_n[...] = joined(plain_f, npart[...], pair_n[...])
    recv_n[chip] = send_n[...]
    to_chips(lambda peer: send_n, recv_n, BN)
    to_partner(part.at[other_rows], pair_f, PF).wait_recv()
    chip_value(plain_f, part, pair_f, stage, send1_f, recv1_f, F1)

    local_sum[...] = jnp.zeros_like(local_sum)

    def shares(h):
        share = sigmoid_row(gate[h])
        return share, 1.0 - share

    def attend(h, i):
        count = (i + 1) * BQ
        here = cols(h)
        queries = pl.ds(i * BQ, BQ)
        keys = pl.ds(0, count)
        local_share = shares(h)[1][:, :1]
        q_block, g_block = q[queries, here], g[queries, here]
        scores = dot(k[keys, here], q_block, NT) * (HD**-0.5 * math.log2(math.e))
        lead = scores[: count - BQ]
        last = scores[count - BQ :]
        key_ids = lax.broadcasted_iota(jnp.int32, (BQ, BQ), 0)
        query_ids = lax.broadcasted_iota(jnp.int32, (BQ, BQ), 1)
        last = jnp.where(key_ids <= query_ids, last, -1e30)
        scores = jnp.concatenate([lead, last], axis=0) if i else last
        weights = jnp.exp2(scores - jnp.max(scores, axis=0, keepdims=True))
        attention = weights * (1.0 / jnp.sum(weights, axis=0, keepdims=True))
        attention_low = attention.astype(BF16)
        value_dot = dot(v[keys, here], g_block, NT)
        delta = jnp.sum(value_dot * attention, axis=0, keepdims=True)
        score_grad = (attention * ((value_dot - delta) * local_share)).astype(BF16)
        seen = jnp.sum(value_dot * attention_low.astype(F32), axis=0, keepdims=True)
        local_sum[pl.ds(h, 1), :] += seen
        dk = dot(score_grad, q_block, NN)
        dv = dot(attention_low, g_block, NN)
        qg[queries, here] = dot(score_grad, k[keys, here], TN) * HD**-0.5
        if i == blocks - 1:
            kl[keys, here] = dk
            vl[keys, here] = dv
        else:
            kl[keys, here] += dk
            vl[keys, here] += dv

    def grad_to_memory():
        all_pages(recv_n, BN).wait_recv()
        own_doc = doc[2 * chip]

        def add(t, total):
            weight = jnp.where((t < chip) & (doc[2 * t + 1] == own_doc), 1.0, 0.0)
            return total + weight * recv_n[t]

        chip_level = lax.fori_loop(0, chips, add, jnp.zeros((heads, HD), F32))
        plain_part = jnp.where(plain_f, npart[...], pair_n[...])
        nprev[...] = jnp.where(plain_f, chip_level, same_here * (chip_level + plain_part))

        def one(h, carry):
            here = cols(h)
            share = shares(h)[0]
            high, low = split(jnp.broadcast_to(nprev[pl.ds(h, 1), :], (HD, HD)))
            features = qf[:, here]
            recip = 1.0 / (1.0 + (dot(features, high, NT) + dot(features, low, NT)))
            rden[:, here] = recip
            num_grad = g[:, here].astype(F32) * (share * recip)
            gpart[pl.ds(pl.multiple_of(h * HD, HD), HD), :] = halves(dot(features, wide(num_grad), TN))
            return carry

        lax.fori_loop(0, heads, one, 0)
        to_partner(gpart.at[other_rows], pair_b, PB).start()

    def read_memory():
        take_back(mprev, out_f, back_f, F3)
        lane = lax.broadcasted_iota(jnp.int32, (1, HD), 1)
        dpart[heads : heads + 1, :] = jnp.zeros((1, HD), F32)

        def one(h, carry):
            here = cols(h)
            share, local_share = shares(h)
            memory = mprev[pl.ds(pl.multiple_of(h * HD, HD), HD), :]
            features = qf[:, here]
            grads = g[:, here]
            recip = rden[:, here]
            memory_read = halves(dot(features, wide(memory), NN)) * recip
            row_sums = jnp.sum(grads.astype(F32) * memory_read, axis=1, keepdims=True)
            den_grad = -(row_sums * (share * recip))
            dpart[pl.ds(h, 1), :] = jnp.sum(features.astype(F32) * den_grad, axis=0, keepdims=True)
            read_sum = jnp.sum(row_sums, axis=0, keepdims=True)
            local_total = jnp.sum(local_sum[pl.ds(h, 1), :], axis=1, keepdims=True)
            gate_part = share * local_share * (read_sum - local_total)
            dpart[heads : heads + 1, :] += jnp.where(lane == h, gate_part, 0.0)
            high, low = split(memory)
            num_part = (dot(grads, high, NT) + dot(grads, low, NT)) * (share * recip)
            feature_grad = num_part + den_grad * nprev[pl.ds(h, 1), :]
            qg[:, here] += feature_grad * slope(q[:, here].astype(F32))
            return carry

        lax.fori_loop(0, heads, one, 0)
        to_partner(dpart, pair_d, PD).start()

    def spread_small():
        to_partner(dpart, pair_d, PD).wait_recv()
        send_d[0:heads, :] = joined(plain_b, dpart[0:heads, :], pair_d[0:heads, :])
        send_d[heads : heads + 1, :] = dpart[heads : heads + 1, :] + pair_d[heads : heads + 1, :]
        recv_d[chip] = send_d[...]
        to_chips(lambda peer: send_d, recv_d, BD)

    def gather_small():
        all_pages(recv_d, BD).wait_recv()
        own_doc = doc[2 * chip + 1]
        is_gate = lax.broadcasted_iota(jnp.int32, (heads + 1, HD), 0) == heads

        def add(t, total):
            weight = jnp.where((t > chip) & (doc[2 * t] == own_doc), 1.0, 0.0)
            return total + jnp.where(is_gate, 1.0, weight) * recv_d[t]

        total = lax.fori_loop(0, chips, add, jnp.zeros((heads + 1, HD), F32))
        plain_part = jnp.where(plain_b, dpart[...], pair_d[...])
        adjusted = jnp.where(plain_b, total, same_here * (total + plain_part))
        small[...] = jnp.where(is_gate, total, adjusted)

    def per_head(h, carry):
        attend(h, blocks - 1)

        @pl.when(h == 1)
        def _():
            to_partner(gpart.at[other_rows], pair_b, PB).wait_recv()
            chip_value(plain_b, gpart, pair_b, stage, send1_b, recv1_b, B1)
            forward_scan(recv1_f, send2_f, recv2_f, F2)

        @pl.when(h == 2)
        def _():
            backward_scan(recv1_b, send2_b, recv2_b, B2)

        for i in reversed(range(blocks - 1)):
            attend(h, i)

        @pl.when(h == 0)
        def _():
            grad_to_memory()

        return carry

    lax.fori_loop(0, heads, per_head, 0)

    hand_back(plain_f, part, pair_f, recv2_f, stage, out_f, mprev, back_f, F3)
    read_memory()
    spread_small()
    hand_back(plain_b, gpart, pair_b, recv2_b, stage, out_b, later, back_b, B3)
    take_back(later, out_b, back_b, B3)
    gather_small()

    for src, dst, n in (
        (npart, pair_n, PN),
        (part.at[other_rows], pair_f, PF),
        (gpart.at[other_rows], pair_b, PB),
        (dpart, pair_d, PD),
        (out_f, back_f, F3),
        (out_b, back_b, B3),
    ):
        to_partner(src, dst, n).wait_send()
    for buffer, n in (
        (recv_n, BN),
        (recv_d, BD),
        (recv1_f, F1),
        (recv2_f, F2),
        (recv1_b, B1),
        (recv2_b, B2),
    ):
        all_pages(buffer, n).wait_send()


def finish_kernel(heads, gate, later, small, k, v, qg, kl, vl, q_out, k_out, v_out, gate_out):
    q_out[...] = qg[...]
    for h in range(heads):
        here = cols(h)
        memory = later[h * HD : (h + 1) * HD, :]
        high, low = split(memory)
        keys = k[:, here].astype(F32)
        values = v[:, here]
        local_share = 1.0 - sigmoid_row(gate[h])
        grads = dot(values, high, NT) + dot(values, low, NT) + small[h : h + 1, :]
        k_out[:, here] = kl[:, here] * HD**-0.5 + grads * slope(keys)
        features = feature(keys).astype(BF16)
        v_out[:, here] = vl[:, here] * local_share + halves(dot(features, wide(memory), NN))
        gate_out[h] = small[heads, h]


def per_device(chips, queries, key_vectors, value_vectors, out_grad, gate_logit, doc_index):
    tokens, width = queries.shape
    heads = width // HD
    half = heads * HD // 2
    page = half // chips
    hbm = pl.BlockSpec(memory_space=pltpu.HBM)
    vmem = pl.BlockSpec(memory_space=pltpu.VMEM)
    smem = pl.BlockSpec(memory_space=pltpu.SMEM)
    local = jax.ShapeDtypeStruct((tokens, width), F32)
    state = jax.ShapeDtypeStruct((heads * HD, HD), F32)
    pages = pltpu.VMEM((chips, page, HD), F32)
    half_state = pltpu.VMEM((half, HD), F32)
    whole_state = pltpu.VMEM((heads * HD, HD), F32)
    operand = pltpu.VMEM((tokens, width), BF16)
    norms = pltpu.VMEM((heads, HD), F32)
    smalls = pltpu.VMEM((heads + 1, HD), F32)
    qg, kl, vl, later, small = pl.pallas_call(
        functools.partial(main_kernel, chips, heads),
        out_shape=(local, local, local, state, jax.ShapeDtypeStruct((heads + 1, HD), F32)),
        in_specs=[smem, smem, hbm, hbm, hbm, hbm],
        out_specs=[vmem] * 5,
        scratch_shapes=[
            operand,
            operand,
            operand,
            operand,
            operand,
            pltpu.VMEM((tokens, width), F32),
            whole_state,
            whole_state,
            whole_state,
            norms,
            norms,
            smalls,
            pltpu.VMEM((heads, BQ), F32),
            half_state,
            half_state,
            half_state,
            norms,
            smalls,
            pages,
            pages,
            pages,
            pages,
            pages,
            pages,
            pages,
            pages,
            norms,
            pltpu.VMEM((chips, heads, HD), F32),
            smalls,
            pltpu.VMEM((chips, heads + 1, HD), F32),
            half_state,
            half_state,
            half_state,
            half_state,
            pltpu.SemaphoreType.DMA((4,)),
            pltpu.SemaphoreType.DMA((12,)),
            pltpu.SemaphoreType.DMA((12,)),
        ],
        compiler_params=pltpu.CompilerParams(
            collective_id=0, has_side_effects=True, vmem_limit_bytes=36 * 1024 * 1024
        ),
        name="exchange",
    )(doc_index, gate_logit, queries, key_vectors, value_vectors, out_grad)

    block = pl.BlockSpec((BQ, width), lambda i: (i, 0))
    whole = pl.BlockSpec((heads * HD, HD), lambda i: (0, 0))
    return pl.pallas_call(
        functools.partial(finish_kernel, heads),
        grid=(tokens // BQ,),
        out_shape=(local, local, local, jax.ShapeDtypeStruct((heads,), F32)),
        in_specs=[
            smem,
            whole,
            pl.BlockSpec((heads + 1, HD), lambda i: (0, 0)),
            block,
            block,
            block,
            block,
            block,
        ],
        out_specs=[block, block, block, smem],
        compiler_params=pltpu.CompilerParams(vmem_limit_bytes=24 * 1024 * 1024),
        name="finish",
    )(gate_logit, later, small, key_vectors, value_vectors, qg, kl, vl)


def solution(mesh):
    spec = P("seq", "head")
    return jax.shard_map(
        functools.partial(per_device, mesh.shape["seq"] // 2),
        mesh=mesh,
        in_specs=(spec, spec, spec, spec, P("head"), P()),
        out_specs=(spec, spec, spec, P("head")),
        check_vma=False,
    )
```

time: 304 us -> 50.9 us (0.17)
  matrix products: 77.1 us -> 0 us
  blocking collectives: 62.8 us -> 0 us
  between operations: 47.7 us -> 0.65 us
  waiting for transfers between devices: 44.8 us -> 0 us
  Pallas kernels: 0 us -> 44.1 us
  local copies, waits for them, and re-layouts: 34.2 us -> 5.83 us
  other arithmetic: 19.9 us -> 0 us
  loops' own time: 15.5 us -> 0 us
    dot_general x36 -> x0, matrix products: 77.1 us -> none  [the longest x3 11.2 us: head_work(): jnp.dot(attention_low, value_head, preferred_element_type=jnp.float32)]
    all_gather x2 -> x0, waiting for transfers between devices: 44.8 us -> none  [gathered_once(): both, at, found = (lax.all_gather(jnp.concatenate(lines), axis), 0, {})]
    pallas_call x0 -> x2, Pallas kernels: none -> 44.1 us  [the longest x1 40.4 us: per_device(): pl.pallas_call(functools.partial(main_kernel, chips, heads), out_shape=(l...]
    all_gather x4 -> x0, blocking collectives: 33.8 us -> none  [gathered_once(): both, at, found = (lax.all_gather(jnp.concatenate(lines), axis), 0, {})]
    psum x3 -> x0, blocking collectives: 29 us -> none  [by_axis(): value = lax.psum(value, axis)]
    another operation x1 -> x0, loops' own time: 15.5 us -> none  [per_device(): results = lax.map(one_head, jnp.arange(head_count, dtype=jnp.int32))]
    dynamic_slice x13 -> x0, local copies, waits for them, and re-layouts: 9.03 us -> none  [the longest x6 3.92 us: take_columns(): lax.dynamic_slice_in_dim(matrix, head_index * head_size, head_size, 1)]
    dynamic_update_slice x21 -> x0, local copies, waits for them, and re-layouts: 7.87 us -> none  [per_device(): results = lax.map(one_head, jnp.arange(head_count, dtype=jnp.int32))]
  transfers between devices with their start and end apart: 2 -> 0, of which waited for: 2 -> 0; matrix products, arithmetic and copies ran while one was open for 2% -> 0% of each run, Pallas kernels for 0% -> 0%
where the time goes in v1:
time: 50.9 us; the launch traced here: 50.6 us
  Pallas kernels  44.1 us (87%)
  local copies, waits for them, and re-layouts  5.83 us (11%)
  between operations  0.65 us (1%)
    pallas_call x1, Pallas kernels, per_device(): pl.pallas_call(functools.partial(main_kernel, chips, heads), out_shape=(l...  40.4 us
    unnamed x12, local copies, waits for them, and re-layouts  5.83 us
    pallas_call x1, Pallas kernels, per_device(): pl.pallas_call(functools.partial(finish_kernel, heads), grid=(tokens // B...  3.74 us

profile of v1, /device:TPU:8, one launch (start us, length us, event | category | flops | bytes accessed | tf_op | source)
XLA Modules:
  0.0 50.6 jit_solution(7934226725854515279)
XLA Ops:
  0.6 0.0 copy-start
  0.6 1.1 %copy-done = bf16[1024,384]{1,0:T(8,128)(2,1)S(1)} copy-done((bf16[1024,384]{1,0:T(8,128)(2,1)S(1)}, bf16[1024,384]{1,0:T(8,128)(2,1)}, u32[]{:S(2)}) %copy-start) | copy-done | bytes 786456
  1.8 0.0 copy-start.1
  1.8 1.1 %copy-done.1 = bf16[1024,384]{1,0:T(8,128)(2,1)S(1)} copy-done((bf16[1024,384]{1,0:T(8,128)(2,1)S(1)}, bf16[1024,384]{1,0:T(8,128)(2,1)}, u32[]{:S(2)}) %copy-start.1) | copy-done | bytes 786456
  2.9 0.0 copy-start.2
  2.9 1.1 %copy-done.2 = bf16[1024,384]{1,0:T(8,128)(2,1)S(1)} copy-done((bf16[1024,384]{1,0:T(8,128)(2,1)S(1)}, bf16[1024,384]{1,0:T(8,128)(2,1)}, u32[]{:S(2)}) %copy-start.2) | copy-done | bytes 786456
  4.0 0.0 copy-start.3
  4.0 1.1 %copy-done.3 = bf16[1024,384]{1,0:T(8,128)(2,1)S(1)} copy-done((bf16[1024,384]{1,0:T(8,128)(2,1)S(1)}, bf16[1024,384]{1,0:T(8,128)(2,1)}, u32[]{:S(2)}) %copy-start.3) | copy-done | bytes 786456
  5.2 0.0 copy-start.4
  5.2 0.7 %copy-done.4 = f32[3]{0:T(128)S(1)} copy-done((f32[3]{0:T(128)S(1)}, f32[3]{0:T(128)}, u32[]{:S(2)}) %copy-start.4) | copy-done | bytes 36
  5.8 0.0 copy-start.5
  5.8 0.7 %copy-done.5 = s32[64]{0:T(128)S(1)} copy-done((s32[64]{0:T(128)S(1)}, s32[64]{0:T(128)}, u32[]{:S(2)}) %copy-start.5) | copy-done | bytes 280
  6.5 40.4 %exchange.1 = (f32[1024,384]{1,0:T(8,128)S(1)}, f32[1024,384]{1,0:T(8,128)S(1)}, f32[1024,384]{1,0:T(8,128)S(1)}, f32[384,128]{1,0:T(8,128)S(1)}, f32[4,128]{1,0:T(4,128)S(1)}) custom-call(s32[64]{0:T(128)S(1)} %copy-done.5, f32[3]{0:T(128)S(1)} %copy-done.4, bf16[1024,384]{1,0:T(8,128)(2,1)S(1)} %copy-done.2, bf16[1024,384]{1,0:T(8,128)(2,1)S(1)} %copy-done, ...), custom_call_target="tpu_custom_call" | custom-call | tf_op jit(solution)/shard_map/exchange/pallas_call | solution.py:461
  46.9 3.7 %finish.1 = (f32[1024,384]{1,0:T(8,128)}, f32[1024,384]{1,0:T(8,128)}, f32[1024,384]{1,0:T(8,128)}, f32[3]{0:T(128)}) custom-call(f32[3]{0:T(128)S(1)} %copy-done.4, f32[384,128]{1,0:T(8,128)S(1)} %get-tuple-element.9.later, f32[4,128]{1,0:T(4,128)S(1)} %get-tuple-element.10.small, bf16[1024,384]{1,0:T(8,128)(2,1)S(1)} %copy-done, ...), custom_call_target="tpu_custom_call" | custom-call | tf_op jit(solution)/shard_map/finish/pallas_call | solution.py:513
Async XLA Ops:
  0.6 1.1 %copy-start = (bf16[1024,384]{1,0:T(8,128)(2,1)S(1)}, bf16[1024,384]{1,0:T(8,128)(2,1)}, u32[]{:S(2)}) copy-start(bf16[1024,384]{1,0:T(8,128)(2,1)} %k.1) | copy-start | bytes 2359300
  1.8 1.1 %copy-start.1 = (bf16[1024,384]{1,0:T(8,128)(2,1)S(1)}, bf16[1024,384]{1,0:T(8,128)(2,1)}, u32[]{:S(2)}) copy-start(bf16[1024,384]{1,0:T(8,128)(2,1)} %v.1) | copy-start | bytes 2359300
  2.9 1.1 %copy-start.2 = (bf16[1024,384]{1,0:T(8,128)(2,1)S(1)}, bf16[1024,384]{1,0:T(8,128)(2,1)}, u32[]{:S(2)}) copy-start(bf16[1024,384]{1,0:T(8,128)(2,1)} %q_hbm.1) | copy-start | bytes 2359300
  4.0 1.1 %copy-start.3 = (bf16[1024,384]{1,0:T(8,128)(2,1)S(1)}, bf16[1024,384]{1,0:T(8,128)(2,1)}, u32[]{:S(2)}) copy-start(bf16[1024,384]{1,0:T(8,128)(2,1)} %g_hbm.1) | copy-start | bytes 2359300
  5.2 0.7 %copy-start.4 = (f32[3]{0:T(128)S(1)}, f32[3]{0:T(128)}, u32[]{:S(2)}) copy-start(f32[3]{0:T(128)} %gate.3) | copy-start | bytes 40
  5.8 0.7 %copy-start.5 = (s32[64]{0:T(128)S(1)}, s32[64]{0:T(128)}, u32[]{:S(2)}) copy-start(s32[64]{0:T(128)} %doc.1) | copy-start | bytes 772

commit v2 on v1

--- a/solution.py
+++ b/solution.py
@@ -41,6 +41,19 @@
 
 def halves(y):
     return y[:, :HD] + y[:, HD:]
+
+
+def row_product(row, matrix):
+    high, low = (jnp.broadcast_to(x, (16, x.shape[1])) for x in split(row))
+    return (dot(high, matrix, NN) + dot(low, matrix, NN))[:1]
+
+
+def flipped(x):
+    return jnp.transpose(x)
+
+
+def state_rows(h):
+    return pl.ds(pl.multiple_of(h * HD, HD), HD)
 
 
 def sigmoid_row(x):
@@ -72,7 +85,10 @@
     v,
     g,
     qf,
-    rden,
+    qf_t,
+    g_t,
+    recip_rows,
+    den_rows,
     part,
     gpart,
     mprev,
@@ -260,6 +276,8 @@
     to_chips(lambda peer: send_n, recv_n, BN)
     to_partner(part.at[other_rows], pair_f, PF).wait_recv()
     chip_value(plain_f, part, pair_f, stage, send1_f, recv1_f, F1)
+    for h in range(heads):
+        qf_t[h * HD : (h + 1) * HD, :] = flipped(qf[:, cols(h)])
 
     local_sum[...] = jnp.zeros_like(local_sum)
 
@@ -311,48 +329,61 @@
         plain_part = jnp.where(plain_f, npart[...], pair_n[...])
         nprev[...] = jnp.where(plain_f, chip_level, same_here * (chip_level + plain_part))
 
-        def one(h, carry):
-            here = cols(h)
-            share = shares(h)[0]
-            high, low = split(jnp.broadcast_to(nprev[pl.ds(h, 1), :], (HD, HD)))
-            features = qf[:, here]
-            recip = 1.0 / (1.0 + (dot(features, high, NT) + dot(features, low, NT)))
-            rden[:, here] = recip
-            num_grad = g[:, here].astype(F32) * (share * recip)
-            gpart[pl.ds(pl.multiple_of(h * HD, HD), HD), :] = halves(dot(features, wide(num_grad), TN))
+        def one(n, carry):
+            h = jnp.where(core == 0, heads - 1 - n, n)
+            share = shares(h)[0][:, :1]
+            features = qf_t[state_rows(h), :]
+            recip = 1.0 / (1.0 + row_product(nprev[pl.ds(h, 1), :], features))
+            recip_rows[pl.ds(h, 1), :] = recip
+            high, low = split(features.astype(F32) * (share * recip))
+            grads = g[:, cols(h)]
+            gpart[state_rows(h), :] = dot(high, grads, NN) + dot(low, grads, NN)
+
+            @pl.when(n == heads // 2)
+            def _():
+                to_partner(gpart.at[other_rows], pair_b, PB).start()
+
             return carry
 
         lax.fori_loop(0, heads, one, 0)
-        to_partner(gpart.at[other_rows], pair_b, PB).start()
 
     def read_memory():
-        take_back(mprev, out_f, back_f, F3)
         lane = lax.broadcasted_iota(jnp.int32, (1, HD), 1)
         dpart[heads : heads + 1, :] = jnp.zeros((1, HD), F32)
 
         def one(h, carry):
-            here = cols(h)
             share, local_share = shares(h)
-            memory = mprev[pl.ds(pl.multiple_of(h * HD, HD), HD), :]
-            features = qf[:, here]
-            grads = g[:, here]
-            recip = rden[:, here]
-            memory_read = halves(dot(features, wide(memory), NN)) * recip
-            row_sums = jnp.sum(grads.astype(F32) * memory_read, axis=1, keepdims=True)
-            den_grad = -(row_sums * (share * recip))
-            dpart[pl.ds(h, 1), :] = jnp.sum(features.astype(F32) * den_grad, axis=0, keepdims=True)
-            read_sum = jnp.sum(row_sums, axis=0, keepdims=True)
+            high, low = split(mprev[state_rows(h), :])
+            features = qf_t[state_rows(h), :]
+            recip = recip_rows[pl.ds(h, 1), :]
+            numerator = dot(high, features, TN) + dot(low, features, TN)
+            products = g_t[state_rows(h), :].astype(F32) * numerator
+            row_sums = jnp.sum(products, axis=0, keepdims=True) * recip
+            den_grad = -(row_sums * (share[:, :1] * recip))
+            den_rows[pl.ds(h, 1), :] = den_grad
+            dpart[pl.ds(h, 1), :] = row_product(den_grad, qf[:, cols(h)])
+            read_sum = jnp.sum(row_sums, axis=1, keepdims=True)
             local_total = jnp.sum(local_sum[pl.ds(h, 1), :], axis=1, keepdims=True)
             gate_part = share * local_share * (read_sum - local_total)
             dpart[heads : heads + 1, :] += jnp.where(lane == h, gate_part, 0.0)
-            high, low = split(memory)
-            num_part = (dot(grads, high, NT) + dot(grads, low, NT)) * (share * recip)
-            feature_grad = num_part + den_grad * nprev[pl.ds(h, 1), :]
-            qg[:, here] += feature_grad * slope(q[:, here].astype(F32))
             return carry
 
         lax.fori_loop(0, heads, one, 0)
         to_partner(dpart, pair_d, PD).start()
+
+    def query_memory_grad():
+        def one(h, carry):
+            here = cols(h)
+            high, low = split(mprev[state_rows(h), :])
+            grads = g_t[state_rows(h), :]
+            factor = shares(h)[0][:, :1] * recip_rows[pl.ds(h, 1), :]
+            norm = jnp.transpose(jnp.broadcast_to(nprev[pl.ds(h, 1), :], (HD, HD)))[:, :1]
+            feature_grad = (dot(high, grads, NN) + dot(low, grads, NN)) * factor
+            feature_grad += norm * den_rows[pl.ds(h, 1), :]
+            qg[:, here] += jnp.transpose(feature_grad) * slope(q[:, here].astype(F32))
+            return carry
+
+        lax.fori_loop(0, heads, one, 0)
 
     def spread_small():
         to_partner(dpart, pair_d, PD).wait_recv()
@@ -376,35 +407,31 @@
         small[...] = jnp.where(is_gate, total, adjusted)
 
     def per_head(h, carry):
-        attend(h, blocks - 1)
-
-        @pl.when(h == 1)
-        def _():
-            to_partner(gpart.at[other_rows], pair_b, PB).wait_recv()
-            chip_value(plain_b, gpart, pair_b, stage, send1_b, recv1_b, B1)
-            forward_scan(recv1_f, send2_f, recv2_f, F2)
-
-        @pl.when(h == 2)
-        def _():
-            backward_scan(recv1_b, send2_b, recv2_b, B2)
-
-        for i in reversed(range(blocks - 1)):
+        for i in reversed(range(blocks)):
             attend(h, i)
 
         @pl.when(h == 0)
         def _():
             grad_to_memory()
+            forward_scan(recv1_f, send2_f, recv2_f, F2)
+            to_partner(gpart.at[other_rows], pair_b, PB).wait_recv()
+            chip_value(plain_b, gpart, pair_b, stage, send1_b, recv1_b, B1)
+            for n in range(heads):
+                g_t[n * HD : (n + 1) * HD, :] = flipped(g[:, cols(n)])
 
         return carry
 
     lax.fori_loop(0, heads, per_head, 0)
 
     hand_back(plain_f, part, pair_f, recv2_f, stage, out_f, mprev, back_f, F3)
+    backward_scan(recv1_b, send2_b, recv2_b, B2)
+    take_back(mprev, out_f, back_f, F3)
     read_memory()
     spread_small()
+    query_memory_grad()
     hand_back(plain_b, gpart, pair_b, recv2_b, stage, out_b, later, back_b, B3)
+    gather_small()
     take_back(later, out_b, back_b, B3)
-    gather_small()
 
     for src, dst, n in (
         (npart, pair_n, PN),
@@ -426,20 +453,35 @@
         all_pages(buffer, n).wait_send()
 
 
-def finish_kernel(heads, gate, later, small, k, v, qg, kl, vl, q_out, k_out, v_out, gate_out):
-    q_out[...] = qg[...]
+def finish_kernel(
+    heads, gate, later, small, k, v, qg, kl, vl, q_out, k_out, v_out, gate_out, k_rows, v_rows, sems
+):
+    blocks = k.shape[0] // BQ
+    copies = [pltpu.make_async_copy(qg, q_out, sems.at[0])]
+    copies[0].start()
+    for i in range(blocks):
+        rows = pl.ds(i * BQ, BQ)
+        for h in range(heads):
+            here = cols(h)
+            memory = later[h * HD : (h + 1) * HD, :]
+            high, low = split(memory)
+            keys = k[rows, here].astype(F32)
+            values = v[rows, here]
+            local_share = 1.0 - sigmoid_row(gate[h])
+            grads = dot(values, high, NT) + dot(values, low, NT) + small[h : h + 1, :]
+            k_rows[rows, here] = kl[rows, here] * HD**-0.5 + grads * slope(keys)
+            features = feature(keys).astype(BF16)
+            v_rows[rows, here] = vl[rows, here] * local_share + halves(
+                dot(features, wide(memory), NN)
+            )
+        for n, (buffer, out) in enumerate(((k_rows, k_out), (v_rows, v_out))):
+            copy = pltpu.make_async_copy(buffer.at[rows], out.at[rows], sems.at[1 + 2 * i + n])
+            copy.start()
+            copies.append(copy)
     for h in range(heads):
-        here = cols(h)
-        memory = later[h * HD : (h + 1) * HD, :]
-        high, low = split(memory)
-        keys = k[:, here].astype(F32)
-        values = v[:, here]
-        local_share = 1.0 - sigmoid_row(gate[h])
-        grads = dot(values, high, NT) + dot(values, low, NT) + small[h : h + 1, :]
-        k_out[:, here] = kl[:, here] * HD**-0.5 + grads * slope(keys)
-        features = feature(keys).astype(BF16)
-        v_out[:, here] = vl[:, here] * local_share + halves(dot(features, wide(memory), NN))
         gate_out[h] = small[heads, h]
+    for copy in copies:
+        copy.wait()
 
 
 def per_device(chips, queries, key_vectors, value_vectors, out_grad, gate_logit, doc_index):
@@ -458,6 +500,7 @@
     operand = pltpu.VMEM((tokens, width), BF16)
     norms = pltpu.VMEM((heads, HD), F32)
     smalls = pltpu.VMEM((heads + 1, HD), F32)
+    operands = (doc_index, gate_logit, queries, key_vectors, value_vectors, out_grad)
     qg, kl, vl, later, small = pl.pallas_call(
         functools.partial(main_kernel, chips, heads),
         out_shape=(local, local, local, state, jax.ShapeDtypeStruct((heads + 1, HD), F32)),
@@ -469,7 +512,10 @@
             operand,
             operand,
             operand,
-            pltpu.VMEM((tokens, width), F32),
+            pltpu.VMEM((width, tokens), BF16),
+            pltpu.VMEM((width, tokens), BF16),
+            pltpu.VMEM((heads, tokens), F32),
+            pltpu.VMEM((heads, tokens), F32),
             whole_state,
             whole_state,
             whole_state,
@@ -506,25 +552,18 @@
             collective_id=0, has_side_effects=True, vmem_limit_bytes=36 * 1024 * 1024
         ),
         name="exchange",
-    )(doc_index, gate_logit, queries, key_vectors, value_vectors, out_grad)
-
-    block = pl.BlockSpec((BQ, width), lambda i: (i, 0))
-    whole = pl.BlockSpec((heads * HD, HD), lambda i: (0, 0))
+    )(*(pltpu.with_memory_space_constraint(x, pltpu.HBM) for x in operands))
+
     return pl.pallas_call(
         functools.partial(finish_kernel, heads),
-        grid=(tokens // BQ,),
         out_shape=(local, local, local, jax.ShapeDtypeStruct((heads,), F32)),
-        in_specs=[
-            smem,
-            whole,
-            pl.BlockSpec((heads + 1, HD), lambda i: (0, 0)),
-            block,
-            block,
-            block,
-            block,
-            block,
+        in_specs=[smem] + [vmem] * 7,
+        out_specs=[hbm, hbm, hbm, smem],
+        scratch_shapes=[
+            pltpu.VMEM((tokens, width), F32),
+            pltpu.VMEM((tokens, width), F32),
+            pltpu.SemaphoreType.DMA((1 + 2 * (tokens // BQ),)),
         ],
-        out_specs=[block, block, block, smem],
         compiler_params=pltpu.CompilerParams(vmem_limit_bytes=24 * 1024 * 1024),
         name="finish",
     )(gate_logit, later, small, key_vectors, value_vectors, qg, kl, vl)

time: 50.9 us -> 42.5 us (0.83)
  local copies, waits for them, and re-layouts: 5.83 us -> 0.01 us
  Pallas kernels: 44.1 us -> 41.4 us
    unnamed x12 -> x6, local copies, waits for them, and re-layouts: 5.83 us -> 0.01 us
    pallas_call x1, Pallas kernels: 40.4 us -> 38.1 us  [per_device(): pl.pallas_call(functools.partial(main_kernel, chips, heads), out_shape=(l...]
where the time goes in v2:
time: 42.5 us; the launch traced here: 42.1 us
  Pallas kernels  41.4 us (97%)
  between operations  0.69 us (2%)
    pallas_call x1, Pallas kernels, per_device(): pl.pallas_call(functools.partial(main_kernel, chips, heads), out_shape=(l...  38.1 us
    pallas_call x1, Pallas kernels, per_device(): pl.pallas_call(functools.partial(finish_kernel, heads), out_shape=(local,...  3.3 us

profile of v2, /device:TPU:8, one launch (start us, length us, event | category | flops | bytes accessed | tf_op | source)
XLA Modules:
  0.0 42.1 jit_solution(12588800766535136767)
XLA Ops:
  0.6 0.0 copy-start.2
  0.6 0.0 copy-start.1
  0.7 0.0 copy-start
  0.7 38.1 %exchange.1 = (f32[1024,384]{1,0:T(8,128)S(1)}, f32[1024,384]{1,0:T(8,128)S(1)}, f32[1024,384]{1,0:T(8,128)S(1)}, f32[384,128]{1,0:T(8,128)S(1)}, f32[4,128]{1,0:T(4,128)S(1)}) custom-call(s32[64]{0:T(128)} %doc.1, f32[3]{0:T(128)} %gate.3, bf16[1024,384]{1,0:T(8,128)(2,1)} %q_hbm.1, bf16[1024,384]{1,0:T(8,128)(2,1)} %k.1, bf16[1024,384]{1,0:T(8,128)(2,1)} %v.1, ...), custom_call_target="tpu_custom_call" | custom-call | tf_op jit(solution)/shard_map/exchange/pallas_call | solution.py:504
  38.8 0.0 copy-done.2
  38.8 0.0 copy-done.1
  38.8 0.0 copy-done
  38.8 3.3 %finish.1 = (f32[1024,384]{1,0:T(8,128)}, f32[1024,384]{1,0:T(8,128)}, f32[1024,384]{1,0:T(8,128)}, f32[3]{0:T(128)}) custom-call(f32[3]{0:T(128)S(1)} %copy-done.2, f32[384,128]{1,0:T(8,128)S(1)} %get-tuple-element.9.later, f32[4,128]{1,0:T(4,128)S(1)} %get-tuple-element.10.small, bf16[1024,384]{1,0:T(8,128)(2,1)S(1)} %copy-done, ...), custom_call_target="tpu_custom_call" | custom-call | tf_op jit(solution)/shard_map/finish/pallas_call | solution.py:557
Async XLA Ops:
  0.6 38.1 %copy-start.2 = (f32[3]{0:T(128)S(1)}, f32[3]{0:T(128)}, u32[]{:S(2)}) copy-start(f32[3]{0:T(128)} %gate.3) | copy-start | bytes 40
  0.6 38.1 %copy-start.1 = (bf16[1024,384]{1,0:T(8,128)(2,1)S(1)}, bf16[1024,384]{1,0:T(8,128)(2,1)}, u32[]{:S(2)}) copy-start(bf16[1024,384]{1,0:T(8,128)(2,1)} %v.1) | copy-start | bytes 2359300
  0.7 38.1 %copy-start = (bf16[1024,384]{1,0:T(8,128)(2,1)S(1)}, bf16[1024,384]{1,0:T(8,128)(2,1)}, u32[]{:S(2)}) copy-start(bf16[1024,384]{1,0:T(8,128)(2,1)} %k.1) | copy-start | bytes 2359300

commit v3 on v2

--- a/solution.py
+++ b/solution.py
@@ -10,6 +10,7 @@
 
 HD = 128
 BQ = 256
+WIDE = 4
 F32 = jnp.float32
 BF16 = jnp.bfloat16
 MESH = pl.DeviceIdType.MESH
@@ -137,15 +138,20 @@
     for c in copies:
         c.start()
 
+    deep = chips // WIDE
+    peers = [
+        lax.rem(chip // deep + a, WIDE) * deep + lax.rem(chip % deep + b, deep)
+        for _, a, b in sorted(
+            (-min(a, WIDE - a) - min(b, deep - b), a, b) for a in range(WIDE) for b in range(deep)
+        )
+        if a or b
+    ]
+
     barrier = pltpu.get_barrier_semaphore()
+    for peer in peers:
+        there = {"seq": 2 * peer + core}
+        pl.semaphore_signal(barrier, inc=1, device_id=there, device_id_type=MESH)
     pl.semaphore_signal(barrier, inc=1, device_id={"seq": partner}, device_id_type=MESH)
-
-    def greet(i, carry):
-        peer = 2 * lax.rem(chip + 1 + i, chips) + core
-        pl.semaphore_signal(barrier, inc=1, device_id={"seq": peer}, device_id_type=MESH)
-        return carry
-
-    lax.fori_loop(0, chips - 1, greet, 0)
 
     def linked(s):
         before = doc[jnp.maximum(s - 1, 0)]
@@ -168,8 +174,7 @@
         )
 
     def to_chips(source, dst, n):
-        def push(i, carry):
-            peer = lax.rem(chip + 1 + i, chips)
+        for peer in peers:
             pltpu.make_async_remote_copy(
                 src_ref=source(peer),
                 dst_ref=dst.at[chip],
@@ -178,9 +183,6 @@
                 device_id={"seq": 2 * peer + core},
                 device_id_type=MESH,
             ).start()
-            return carry
-
-        lax.fori_loop(0, chips - 1, push, 0)
 
     def all_pages(buffer, n):
         rest = buffer.at[pl.ds(0, chips - 1)]
@@ -278,8 +280,6 @@
     chip_value(plain_f, part, pair_f, stage, send1_f, recv1_f, F1)
     for h in range(heads):
         qf_t[h * HD : (h + 1) * HD, :] = flipped(qf[:, cols(h)])
-
-    local_sum[...] = jnp.zeros_like(local_sum)
 
     def shares(h):
         share = sigmoid_row(gate[h])
@@ -305,8 +305,6 @@
         value_dot = dot(v[keys, here], g_block, NT)
         delta = jnp.sum(value_dot * attention, axis=0, keepdims=True)
         score_grad = (attention * ((value_dot - delta) * local_share)).astype(BF16)
-        seen = jnp.sum(value_dot * attention_low.astype(F32), axis=0, keepdims=True)
-        local_sum[pl.ds(h, 1), :] += seen
         dk = dot(score_grad, q_block, NN)
         dv = dot(attention_low, g_block, NN)
         qg[queries, here] = dot(score_grad, k[keys, here], TN) * HD**-0.5
@@ -409,6 +407,8 @@
     def per_head(h, carry):
         for i in reversed(range(blocks)):
             attend(h, i)
+        here = cols(h)
+        local_sum[pl.ds(h, 1), :] = jnp.sum(v[:, here].astype(F32) * vl[:, here], axis=0, keepdims=True)
 
         @pl.when(h == 0)
         def _():
@@ -522,7 +522,7 @@
             norms,
             norms,
             smalls,
-            pltpu.VMEM((heads, BQ), F32),
+            pltpu.VMEM((heads, HD), F32),
             half_state,
             half_state,
             half_state,

time: 42.5 us -> 40.9 us (0.962)
  Pallas kernels: 41.4 us -> 39.8 us
    pallas_call x1, Pallas kernels: 38.1 us -> 36.5 us  [per_device(): pl.pallas_call(functools.partial(main_kernel, chips, heads), out_shape=(l...]
where the time goes in v3:
time: 40.9 us; the launch traced here: 40.5 us
  Pallas kernels  39.8 us (97%)
  between operations  0.69 us (2%)
    pallas_call x1, Pallas kernels, per_device(): pl.pallas_call(functools.partial(main_kernel, chips, heads), out_shape=(l...  36.5 us
    pallas_call x1, Pallas kernels, per_device(): pl.pallas_call(functools.partial(finish_kernel, heads), out_shape=(local,...  3.3 us

profile of v3, /device:TPU:8, one launch (start us, length us, event | category | flops | bytes accessed | tf_op | source)
XLA Modules:
  0.0 40.5 jit_solution(14030462074504474858)
XLA Ops:
  0.6 0.0 copy-start.2
  0.6 0.0 copy-start.1
  0.7 0.0 copy-start
  0.7 36.5 %exchange.1 = (f32[1024,384]{1,0:T(8,128)S(1)}, f32[1024,384]{1,0:T(8,128)S(1)}, f32[1024,384]{1,0:T(8,128)S(1)}, f32[384,128]{1,0:T(8,128)S(1)}, f32[4,128]{1,0:T(4,128)S(1)}) custom-call(s32[64]{0:T(128)} %doc.1, f32[3]{0:T(128)} %gate.3, bf16[1024,384]{1,0:T(8,128)(2,1)} %q_hbm.1, bf16[1024,384]{1,0:T(8,128)(2,1)} %k.1, bf16[1024,384]{1,0:T(8,128)(2,1)} %v.1, ...), custom_call_target="tpu_custom_call" | custom-call | tf_op jit(solution)/shard_map/exchange/pallas_call | solution.py:504
  37.2 0.0 copy-done.2
  37.2 0.0 copy-done.1
  37.2 0.0 copy-done
  37.2 3.3 %finish.1 = (f32[1024,384]{1,0:T(8,128)}, f32[1024,384]{1,0:T(8,128)}, f32[1024,384]{1,0:T(8,128)}, f32[3]{0:T(128)}) custom-call(f32[3]{0:T(128)S(1)} %copy-done.2, f32[384,128]{1,0:T(8,128)S(1)} %get-tuple-element.9.later, f32[4,128]{1,0:T(4,128)S(1)} %get-tuple-element.10.small, bf16[1024,384]{1,0:T(8,128)(2,1)S(1)} %copy-done, ...), custom_call_target="tpu_custom_call" | custom-call | tf_op jit(solution)/shard_map/finish/pallas_call | solution.py:557
Async XLA Ops:
  0.6 36.5 %copy-start.2 = (f32[3]{0:T(128)S(1)}, f32[3]{0:T(128)}, u32[]{:S(2)}) copy-start(f32[3]{0:T(128)} %gate.3) | copy-start | bytes 40
  0.6 36.5 %copy-start.1 = (bf16[1024,384]{1,0:T(8,128)(2,1)S(1)}, bf16[1024,384]{1,0:T(8,128)(2,1)}, u32[]{:S(2)}) copy-start(bf16[1024,384]{1,0:T(8,128)(2,1)} %v.1) | copy-start | bytes 2359300
  0.7 36.5 %copy-start = (bf16[1024,384]{1,0:T(8,128)(2,1)S(1)}, bf16[1024,384]{1,0:T(8,128)(2,1)}, u32[]{:S(2)}) copy-start(bf16[1024,384]{1,0:T(8,128)(2,1)} %k.1) | copy-start | bytes 2359300

commit v4 on v3

--- a/solution.py
+++ b/solution.py
@@ -154,12 +154,13 @@
     pl.semaphore_signal(barrier, inc=1, device_id={"seq": partner}, device_id_type=MESH)
 
     def linked(s):
-        before = doc[jnp.maximum(s - 1, 0)]
+        before = doc[max(s - 1, 0) if isinstance(s, int) else jnp.maximum(s - 1, 0)]
         return jnp.where((s > 0) & (before == doc[s]), 1.0, 0.0)
 
     def linked_next(s):
-        after = doc[jnp.minimum(s + 1, 2 * chips - 1)]
-        return jnp.where((s < 2 * chips - 1) & (after == doc[s]), 1.0, 0.0)
+        last = 2 * chips - 1
+        after = doc[min(s + 1, last) if isinstance(s, int) else jnp.minimum(s + 1, last)]
+        return jnp.where((s < last) & (after == doc[s]), 1.0, 0.0)
 
     same_here = linked(2 * chip + 1)
 
@@ -219,7 +220,9 @@
             send2[t] = before
             return recv1[t] + linked(2 * t + 1) * before
 
-        lax.fori_loop(0, chips, step, jnp.zeros((page, HD), F32))
+        run = jnp.zeros((page, HD), F32)
+        for i in range(chips):
+            run = step(i, run)
         recv2[chip] = send2[chip]
         to_chips(lambda peer: send2.at[peer], recv2, n)
 
@@ -232,7 +235,9 @@
             send2[t] = after
             return recv1[t] + linked_next(2 * t) * after
 
-        lax.fori_loop(0, chips, step, jnp.zeros((page, HD), F32))
+        run = jnp.zeros((page, HD), F32)
+        for i in range(chips):
+            run = step(i, run)
         recv2[chip] = send2[chip]
         to_chips(lambda peer: send2.at[peer], recv2, n)
 
@@ -280,6 +285,7 @@
     chip_value(plain_f, part, pair_f, stage, send1_f, recv1_f, F1)
     for h in range(heads):
         qf_t[h * HD : (h + 1) * HD, :] = flipped(qf[:, cols(h)])
+        g_t[h * HD : (h + 1) * HD, :] = flipped(g[:, cols(h)])
 
     def shares(h):
         share = sigmoid_row(gate[h])
@@ -323,7 +329,9 @@
             weight = jnp.where((t < chip) & (doc[2 * t + 1] == own_doc), 1.0, 0.0)
             return total + weight * recv_n[t]
 
-        chip_level = lax.fori_loop(0, chips, add, jnp.zeros((heads, HD), F32))
+        chip_level = jnp.zeros((heads, HD), F32)
+        for t in range(chips):
+            chip_level = add(t, chip_level)
         plain_part = jnp.where(plain_f, npart[...], pair_n[...])
         nprev[...] = jnp.where(plain_f, chip_level, same_here * (chip_level + plain_part))
 
@@ -349,7 +357,13 @@
         lane = lax.broadcasted_iota(jnp.int32, (1, HD), 1)
         dpart[heads : heads + 1, :] = jnp.zeros((1, HD), F32)
 
-        def one(h, carry):
+        def one(n, carry):
+            h = jnp.where(core == 0, n, heads - 1 - n)
+
+            @pl.when(n == 1)
+            def _():
+                take_back(mprev, out_f, back_f, F3)
+
             share, local_share = shares(h)
             high, low = split(mprev[state_rows(h), :])
             features = qf_t[state_rows(h), :]
@@ -399,7 +413,9 @@
             weight = jnp.where((t > chip) & (doc[2 * t] == own_doc), 1.0, 0.0)
             return total + jnp.where(is_gate, 1.0, weight) * recv_d[t]
 
-        total = lax.fori_loop(0, chips, add, jnp.zeros((heads + 1, HD), F32))
+        total = jnp.zeros((heads + 1, HD), F32)
+        for t in range(chips):
+            total = add(t, total)
         plain_part = jnp.where(plain_b, dpart[...], pair_d[...])
         adjusted = jnp.where(plain_b, total, same_here * (total + plain_part))
         small[...] = jnp.where(is_gate, total, adjusted)
@@ -416,8 +432,6 @@
             forward_scan(recv1_f, send2_f, recv2_f, F2)
             to_partner(gpart.at[other_rows], pair_b, PB).wait_recv()
             chip_value(plain_b, gpart, pair_b, stage, send1_b, recv1_b, B1)
-            for n in range(heads):
-                g_t[n * HD : (n + 1) * HD, :] = flipped(g[:, cols(n)])
 
         return carry
 
@@ -425,7 +439,6 @@
 
     hand_back(plain_f, part, pair_f, recv2_f, stage, out_f, mprev, back_f, F3)
     backward_scan(recv1_b, send2_b, recv2_b, B2)
-    take_back(mprev, out_f, back_f, F3)
     read_memory()
     spread_small()
     query_memory_grad()

time: 40.9 us -> 39.7 us (0.971)
  Pallas kernels: 39.8 us -> 38.3 us
    pallas_call x1, Pallas kernels: 36.5 us -> 35 us  [per_device(): pl.pallas_call(functools.partial(main_kernel, chips, heads), out_shape=(l...]
where the time goes in v4:
time: 39.7 us; the launch traced here: 39 us
  Pallas kernels  38.3 us (96%)
  between operations  0.69 us (2%)
    pallas_call x1, Pallas kernels, per_device(): pl.pallas_call(functools.partial(main_kernel, chips, heads), out_shape=(l...  35 us
    pallas_call x1, Pallas kernels, per_device(): pl.pallas_call(functools.partial(finish_kernel, heads), out_shape=(local,...  3.3 us

profile of v4, /device:TPU:8, one launch (start us, length us, event | category | flops | bytes accessed | tf_op | source)
XLA Modules:
  0.0 39.0 jit_solution(16885202452728493991)
XLA Ops:
  0.6 0.0 copy-start.2
  0.6 0.0 copy-start.1
  0.7 0.0 copy-start
  0.7 35.0 %exchange.1 = (f32[1024,384]{1,0:T(8,128)S(1)}, f32[1024,384]{1,0:T(8,128)S(1)}, f32[1024,384]{1,0:T(8,128)S(1)}, f32[384,128]{1,0:T(8,128)S(1)}, f32[4,128]{1,0:T(4,128)S(1)}) custom-call(s32[64]{0:T(128)} %doc.1, f32[3]{0:T(128)} %gate.3, bf16[1024,384]{1,0:T(8,128)(2,1)} %q_hbm.1, bf16[1024,384]{1,0:T(8,128)(2,1)} %k.1, bf16[1024,384]{1,0:T(8,128)(2,1)} %v.1, ...), custom_call_target="tpu_custom_call" | custom-call | tf_op jit(solution)/shard_map/exchange/pallas_call | solution.py:517
  35.7 0.0 copy-done.2
  35.7 0.0 copy-done.1
  35.7 0.0 copy-done
  35.7 3.3 %finish.1 = (f32[1024,384]{1,0:T(8,128)}, f32[1024,384]{1,0:T(8,128)}, f32[1024,384]{1,0:T(8,128)}, f32[3]{0:T(128)}) custom-call(f32[3]{0:T(128)S(1)} %copy-done.2, f32[384,128]{1,0:T(8,128)S(1)} %get-tuple-element.9.later, f32[4,128]{1,0:T(4,128)S(1)} %get-tuple-element.10.small, bf16[1024,384]{1,0:T(8,128)(2,1)S(1)} %copy-done, ...), custom_call_target="tpu_custom_call" | custom-call | tf_op jit(solution)/shard_map/finish/pallas_call | solution.py:570
Async XLA Ops:
  0.6 35.0 %copy-start.2 = (f32[3]{0:T(128)S(1)}, f32[3]{0:T(128)}, u32[]{:S(2)}) copy-start(f32[3]{0:T(128)} %gate.3) | copy-start | bytes 40
  0.6 35.0 %copy-start.1 = (bf16[1024,384]{1,0:T(8,128)(2,1)S(1)}, bf16[1024,384]{1,0:T(8,128)(2,1)}, u32[]{:S(2)}) copy-start(bf16[1024,384]{1,0:T(8,128)(2,1)} %v.1) | copy-start | bytes 2359300
  0.7 35.0 %copy-start = (bf16[1024,384]{1,0:T(8,128)(2,1)S(1)}, bf16[1024,384]{1,0:T(8,128)(2,1)}, u32[]{:S(2)}) copy-start(bf16[1024,384]{1,0:T(8,128)(2,1)} %k.1) | copy-start | bytes 2359300

commit v5 on v4

--- a/solution.py
+++ b/solution.py
@@ -335,7 +335,7 @@
         plain_part = jnp.where(plain_f, npart[...], pair_n[...])
         nprev[...] = jnp.where(plain_f, chip_level, same_here * (chip_level + plain_part))
 
-        def one(n, carry):
+        def one(n):
             h = jnp.where(core == 0, heads - 1 - n, n)
             share = shares(h)[0][:, :1]
             features = qf_t[state_rows(h), :]
@@ -345,23 +345,20 @@
             grads = g[:, cols(h)]
             gpart[state_rows(h), :] = dot(high, grads, NN) + dot(low, grads, NN)
 
-            @pl.when(n == heads // 2)
-            def _():
+            if n == heads // 2:
                 to_partner(gpart.at[other_rows], pair_b, PB).start()
 
-            return carry
-
-        lax.fori_loop(0, heads, one, 0)
+        for n in range(heads):
+            one(n)
 
     def read_memory():
         lane = lax.broadcasted_iota(jnp.int32, (1, HD), 1)
         dpart[heads : heads + 1, :] = jnp.zeros((1, HD), F32)
 
-        def one(n, carry):
+        def one(n):
             h = jnp.where(core == 0, n, heads - 1 - n)
 
-            @pl.when(n == 1)
-            def _():
+            if n == 1:
                 take_back(mprev, out_f, back_f, F3)
 
             share, local_share = shares(h)
@@ -378,13 +375,12 @@
             local_total = jnp.sum(local_sum[pl.ds(h, 1), :], axis=1, keepdims=True)
             gate_part = share * local_share * (read_sum - local_total)
             dpart[heads : heads + 1, :] += jnp.where(lane == h, gate_part, 0.0)
-            return carry
-
-        lax.fori_loop(0, heads, one, 0)
+        for n in range(heads):
+            one(n)
         to_partner(dpart, pair_d, PD).start()
 
     def query_memory_grad():
-        def one(h, carry):
+        def one(h):
             here = cols(h)
             high, low = split(mprev[state_rows(h), :])
             grads = g_t[state_rows(h), :]
@@ -393,9 +389,8 @@
             feature_grad = (dot(high, grads, NN) + dot(low, grads, NN)) * factor
             feature_grad += norm * den_rows[pl.ds(h, 1), :]
             qg[:, here] += jnp.transpose(feature_grad) * slope(q[:, here].astype(F32))
-            return carry
-
-        lax.fori_loop(0, heads, one, 0)
+        for n in range(heads):
+            one(n)
 
     def spread_small():
         to_partner(dpart, pair_d, PD).wait_recv()

time: 39.7 us -> 39.4 us (level)
  Pallas kernels: 38.3 us -> 37.9 us
where the time goes in v5:
time: 39.4 us; the launch traced here: 38.6 us
  Pallas kernels  37.9 us (96%)
  between operations  0.69 us (2%)
    pallas_call x1, Pallas kernels, per_device(): pl.pallas_call(functools.partial(main_kernel, chips, heads), out_shape=(l...  34.6 us
    pallas_call x1, Pallas kernels, per_device(): pl.pallas_call(functools.partial(finish_kernel, heads), out_shape=(local,...  3.3 us

profile of v5, /device:TPU:8, one launch (start us, length us, event | category | flops | bytes accessed | tf_op | source)
XLA Modules:
  0.0 38.6 jit_solution(5436174044046538331)
XLA Ops:
  0.6 0.0 copy-start.2
  0.6 0.0 copy-start.1
  0.7 0.0 copy-start
  0.7 34.6 %exchange.1 = (f32[1024,384]{1,0:T(8,128)S(1)}, f32[1024,384]{1,0:T(8,128)S(1)}, f32[1024,384]{1,0:T(8,128)S(1)}, f32[384,128]{1,0:T(8,128)S(1)}, f32[4,128]{1,0:T(4,128)S(1)}) custom-call(s32[64]{0:T(128)} %doc.1, f32[3]{0:T(128)} %gate.3, bf16[1024,384]{1,0:T(8,128)(2,1)} %q_hbm.1, bf16[1024,384]{1,0:T(8,128)(2,1)} %k.1, bf16[1024,384]{1,0:T(8,128)(2,1)} %v.1, ...), custom_call_target="tpu_custom_call" | custom-call | tf_op jit(solution)/shard_map/exchange/pallas_call | solution.py:512
  35.3 0.0 copy-done.2
  35.3 0.0 copy-done.1
  35.3 0.0 copy-done
  35.3 3.3 %finish.1 = (f32[1024,384]{1,0:T(8,128)}, f32[1024,384]{1,0:T(8,128)}, f32[1024,384]{1,0:T(8,128)}, f32[3]{0:T(128)}) custom-call(f32[3]{0:T(128)S(1)} %copy-done.2, f32[384,128]{1,0:T(8,128)S(1)} %get-tuple-element.9.later, f32[4,128]{1,0:T(4,128)S(1)} %get-tuple-element.10.small, bf16[1024,384]{1,0:T(8,128)(2,1)S(1)} %copy-done, ...), custom_call_target="tpu_custom_call" | custom-call | tf_op jit(solution)/shard_map/finish/pallas_call | solution.py:565
Async XLA Ops:
  0.6 34.7 %copy-start.2 = (f32[3]{0:T(128)S(1)}, f32[3]{0:T(128)}, u32[]{:S(2)}) copy-start(f32[3]{0:T(128)} %gate.3) | copy-start | bytes 40
  0.6 34.7 %copy-start.1 = (bf16[1024,384]{1,0:T(8,128)(2,1)S(1)}, bf16[1024,384]{1,0:T(8,128)(2,1)}, u32[]{:S(2)}) copy-start(bf16[1024,384]{1,0:T(8,128)(2,1)} %v.1) | copy-start | bytes 2359300
  0.7 34.7 %copy-start = (bf16[1024,384]{1,0:T(8,128)(2,1)S(1)}, bf16[1024,384]{1,0:T(8,128)(2,1)}, u32[]{:S(2)}) copy-start(bf16[1024,384]{1,0:T(8,128)(2,1)} %k.1) | copy-start | bytes 2359300

commit v6 on v5

--- a/solution.py
+++ b/solution.py
@@ -10,6 +10,7 @@
 
 HD = 128
 BQ = 256
+OUT_ROWS = 128
 WIDE = 4
 F32 = jnp.float32
 BF16 = jnp.bfloat16
@@ -464,11 +465,11 @@
 def finish_kernel(
     heads, gate, later, small, k, v, qg, kl, vl, q_out, k_out, v_out, gate_out, k_rows, v_rows, sems
 ):
-    blocks = k.shape[0] // BQ
+    blocks = k.shape[0] // OUT_ROWS
     copies = [pltpu.make_async_copy(qg, q_out, sems.at[0])]
     copies[0].start()
     for i in range(blocks):
-        rows = pl.ds(i * BQ, BQ)
+        rows = pl.ds(i * OUT_ROWS, OUT_ROWS)
         for h in range(heads):
             here = cols(h)
             memory = later[h * HD : (h + 1) * HD, :]
@@ -570,7 +571,7 @@
         scratch_shapes=[
             pltpu.VMEM((tokens, width), F32),
             pltpu.VMEM((tokens, width), F32),
-            pltpu.SemaphoreType.DMA((1 + 2 * (tokens // BQ),)),
+            pltpu.SemaphoreType.DMA((1 + 2 * (tokens // OUT_ROWS),)),
         ],
         compiler_params=pltpu.CompilerParams(vmem_limit_bytes=24 * 1024 * 1024),
         name="finish",

time: 39.4 us -> 39.5 us (level)
  no operation moved by 1% of the time
where the time goes in v6:
time: 39.5 us; the launch traced here: 38.8 us
  Pallas kernels  38.1 us (96%)
  between operations  0.69 us (2%)
    pallas_call x1, Pallas kernels, per_device(): pl.pallas_call(functools.partial(main_kernel, chips, heads), out_shape=(l...  34.6 us
    pallas_call x1, Pallas kernels, per_device(): pl.pallas_call(functools.partial(finish_kernel, heads), out_shape=(local,...  3.48 us

profile of v6, /device:TPU:8, one launch (start us, length us, event | category | flops | bytes accessed | tf_op | source)
XLA Modules:
  0.0 38.8 jit_solution(17508129753737081759)
XLA Ops:
  0.6 0.0 copy-start.2
  0.6 0.0 copy-start.1
  0.7 0.0 copy-start
  0.7 34.6 %exchange.1 = (f32[1024,384]{1,0:T(8,128)S(1)}, f32[1024,384]{1,0:T(8,128)S(1)}, f32[1024,384]{1,0:T(8,128)S(1)}, f32[384,128]{1,0:T(8,128)S(1)}, f32[4,128]{1,0:T(4,128)S(1)}) custom-call(s32[64]{0:T(128)} %doc.1, f32[3]{0:T(128)} %gate.3, bf16[1024,384]{1,0:T(8,128)(2,1)} %q_hbm.1, bf16[1024,384]{1,0:T(8,128)(2,1)} %k.1, bf16[1024,384]{1,0:T(8,128)(2,1)} %v.1, ...), custom_call_target="tpu_custom_call" | custom-call | tf_op jit(solution)/shard_map/exchange/pallas_call | solution.py:513
  35.3 0.0 copy-done.2
  35.3 0.0 copy-done.1
  35.3 0.0 copy-done
  35.3 3.5 %finish.1 = (f32[1024,384]{1,0:T(8,128)}, f32[1024,384]{1,0:T(8,128)}, f32[1024,384]{1,0:T(8,128)}, f32[3]{0:T(128)}) custom-call(f32[3]{0:T(128)S(1)} %copy-done.2, f32[384,128]{1,0:T(8,128)S(1)} %get-tuple-element.9.later, f32[4,128]{1,0:T(4,128)S(1)} %get-tuple-element.10.small, bf16[1024,384]{1,0:T(8,128)(2,1)S(1)} %copy-done, ...), custom_call_target="tpu_custom_call" | custom-call | tf_op jit(solution)/shard_map/finish/pallas_call | solution.py:566
Async XLA Ops:
  0.6 34.7 %copy-start.2 = (f32[3]{0:T(128)S(1)}, f32[3]{0:T(128)}, u32[]{:S(2)}) copy-start(f32[3]{0:T(128)} %gate.3) | copy-start | bytes 40
  0.6 34.7 %copy-start.1 = (bf16[1024,384]{1,0:T(8,128)(2,1)S(1)}, bf16[1024,384]{1,0:T(8,128)(2,1)}, u32[]{:S(2)}) copy-start(bf16[1024,384]{1,0:T(8,128)(2,1)} %v.1) | copy-start | bytes 2359300
  0.7 34.7 %copy-start = (bf16[1024,384]{1,0:T(8,128)(2,1)S(1)}, bf16[1024,384]{1,0:T(8,128)(2,1)}, u32[]{:S(2)}) copy-start(bf16[1024,384]{1,0:T(8,128)(2,1)} %k.1) | copy-start | bytes 2359300
